TPU v7x, 32 devices: a whole 2x2x4 slice. The times are simulated.
32 devices in a mesh: band: 4 (over y, x), lev: 8 (over z, core).
Axes of the slice: x: 2, y: 2, z: 4, core: 2. Of those that a mesh axis runs over, the one named last changes fastest.
Arguments:
- adj_spec: bfloat16 [32, 1280, 2, 1280], P('lev', 'band'), may hold values from -6 to 6
- wave_of_slot: int32 [1280], replicated, may hold values from 0 to 1279, each once
- legendre: bfloat16 [1280, 8, 1280], P('band'), may hold values from -0.15625 to 0.15625
- lat_weight: float32 [8], replicated, may hold values from 0.5 to 1.5
- traj: bfloat16 [32, 16, 5136], P('lev', 'band'), may hold values from -3 to 3
- traj_exp: int32 [32, 16, 4], P('lev', 'band'), may hold values from -2 to 2
- traj_order: int32 [8, 4], P('lev'), may hold values from 0 to 3, each once within a row
- lev_coef: float32 [32], P('lev'), may hold values from 0.02 to 0.2
Outputs:
- adj_out: bfloat16 [32, 1280, 2, 1280], P('lev', 'band')
Inputs may be any that keep to these rules, and one draw needn't show every extreme that they name: `wave_of_slot`: every wavenumber 0 to 1279 is held by exactly one slot. `traj_order`: each row is a permutation of 0 to 3.
All inputs are finite; a program needn't handle non-finite values.
Results may differ from a plain program's by a relative error of at most 0.0085.
Values may be sent and summed in bfloat16 or wider, within the bound.
A program may use at most 128 MiB of HBM per device.

v0:
```python
import functools
import math

import jax
import jax.numpy as jnp
from jax import lax
from jax.experimental import pallas as pl
from jax.experimental.pallas import tpu as pltpu
from jax.sharding import PartitionSpec as P

NBLK = 4
LANES = 128


def slot_step(slots):
    step = 64 if slots % 64 == 0 else slots
    sub = next(width for width in (32, 16, 8, 4, 2, 1) if step % width == 0)
    return step, sub


def split_parity(leg_ref, limit_ref, first, sub):
    table = leg_ref[pl.ds(first, sub)].astype(jnp.float32)
    heights, degrees = table.shape[1], table.shape[2]
    lane = lax.broadcasted_iota(jnp.int32, table.shape, 2)
    limit = jnp.concatenate([limit_ref[pl.ds(first, sub)]] * (degrees // LANES), axis=2)
    table = jnp.where(lane < limit, table, 0.0)
    even = jnp.where(lane % 2 == 0, table, 0.0)
    odd = jnp.where(lane % 2 == 0, 0.0, table)
    rows = sub * heights
    return (
        even.reshape(rows, degrees).astype(jnp.bfloat16),
        odd.reshape(rows, degrees).astype(jnp.bfloat16),
    )


def same_slot(sub, heights, levels):
    shape = (sub, heights, levels * sub * 2)
    held = lax.broadcasted_iota(jnp.int32, shape, 0)
    lane = lax.broadcasted_iota(jnp.int32, shape, 2)
    return held == (lane % (sub * 2)) // 2


def swap_pairs(value):
    lane = lax.broadcasted_iota(jnp.int32, value.shape, 1)
    width = value.shape[1]
    return jnp.where(lane % 2 == 0, pltpu.roll(value, width - 1, 1), pltpu.roll(value, 1, 1))


def synthesis_kernel(step, sub, x_ref, leg_ref, limit_ref, weight_ref, turn_ref, out_ref):
    levels, degrees = x_ref.shape[0], x_ref.shape[3]
    heights = leg_ref.shape[1]
    mask = same_slot(sub, heights, levels)
    width = sub * 2
    north, south = [], []
    for first in range(0, step, sub):
        even, odd = split_parity(leg_ref, limit_ref, first, sub)
        spec = x_ref[:, pl.ds(first, sub)].reshape(levels * width, degrees)
        sums = []
        for table in (even, odd):
            cross = lax.dot_general(
                table, spec, (((1,), (1,)), ((), ())), preferred_element_type=jnp.float32
            ).reshape(sub, heights, levels * width)
            sums.append(jnp.sum(jnp.where(mask, cross, 0.0), axis=0))
        north.append(sums[0] + sums[1])
        south.append(sums[0] - sums[1])
    weight = weight_ref[...][:, :1]
    turn = turn_ref[...]
    bands = out_ref.shape[0]
    pairs = heights // bands
    for side, parts in enumerate((north, south)):
        total = None
        for level in range(levels + 1):
            if level < levels:
                lanes = slice(level * width, (level + 1) * width)
                value = jnp.concatenate([part[:, lanes] for part in parts], axis=1) * weight
                value = value * turn[0:1] + swap_pairs(value) * turn[1:2]
                total = value if total is None else total + value
            else:
                value = total
            sent = value.astype(jnp.bfloat16)
            for band in range(bands):
                rows = slice(level * pairs, (level + 1) * pairs)
                out_ref[band, side, rows] = sent[band * pairs : (band + 1) * pairs]


def analysis_kernel(step, sub, coef_ref, leg_ref, limit_ref, turn_ref, out_ref):
    levels, degrees = out_ref.shape[0], out_ref.shape[3]
    heights = leg_ref.shape[1]
    mask = same_slot(sub, heights, levels)
    width = sub * 2
    turn = turn_ref[...]
    held = coef_ref[...].astype(jnp.float32)
    bands = held.shape[0]
    pairs = heights // bands
    sides = []
    for side in range(2):
        values = []
        for level in range(levels):
            rows = slice(level * pairs, (level + 1) * pairs)
            value = jnp.concatenate([held[band, side, rows] for band in range(bands)], axis=0)
            values.append(value * turn[0:1] - swap_pairs(value) * turn[1:2])
        sides.append(values)
    for index, first in enumerate(range(0, step, sub)):
        tables = split_parity(leg_ref, limit_ref, first, sub)
        lanes = slice(index * width, (index + 1) * width)
        total = None
        for values, table in zip(sides, tables):
            row = jnp.concatenate([value[:, lanes] for value in values], axis=1)
            spread = jnp.where(mask, row[None], 0.0).reshape(sub * heights, levels * width)
            part = lax.dot_general(
                spread.astype(jnp.bfloat16),
                table,
                (((0,), (0,)), ((), ())),
                preferred_element_type=jnp.float32,
            )
            total = part if total is None else total + part
        out_ref[:, pl.ds(first, sub)] = total.astype(jnp.bfloat16).reshape(levels, sub, 2, degrees)


def spectral_call(kernel, slots, operands, specs, out_shape, out_spec, name):
    step, sub = slot_step(slots)
    return pl.pallas_call(
        functools.partial(kernel, step, sub),
        grid=(slots // step,),
        in_specs=specs,
        out_specs=out_spec,
        out_shape=out_shape,
        name=name,
        compiler_params=pltpu.CompilerParams(vmem_limit_bytes=48 * 1024 * 1024),
    )(*operands)


def cos_turn(count, period):
    left = count - jnp.floor(count * (1.0 / period)) * period
    angle = math.pi * (0.5 - jnp.abs(left * (2.0 / period) - 1.0))
    square = angle * angle
    series = 1.0
    for order in (11, 9, 7, 5, 3):
        series = 1.0 - series * square * (1.0 / (order * (order - 1)))
    return -angle * series


def trig_tables(waves, lon_count, width):
    quarter = lon_count // NBLK
    blocks = -(-quarter // LANES)
    period = 2 * lon_count
    wave = jnp.repeat(waves, 2).astype(jnp.float32)[:, None]
    shift = (jnp.arange(wave.shape[0], dtype=jnp.int32) % 2)[:, None] * (lon_count // 2)
    fine = wave * (2 * jnp.arange(LANES, dtype=jnp.int32) + 1).astype(jnp.float32)[None, :]
    coarse = wave * (2 * LANES * jnp.arange(blocks, dtype=jnp.int32)).astype(jnp.float32)[None, :]
    coarse = coarse + shift.astype(jnp.float32)
    quarter_back = 3.0 * (lon_count // 2)
    table = (
        cos_turn(coarse, period)[:, :, None] * cos_turn(fine, period)[:, None, :]
        - cos_turn(coarse + quarter_back, period)[:, :, None]
        * cos_turn(fine + quarter_back, period)[:, None, :]
    )
    return table.astype(jnp.bfloat16).reshape(wave.shape[0], blocks * LANES)


def body(adj_spec, wave_of_slot, legendre, lat_weight, traj, traj_exp, traj_order, lev_coef):
    levels, slots, _, degrees = adj_spec.shape
    heights = legendre.shape[1]
    lat_rows = traj.shape[1]
    pairs = lat_rows // 2
    lon_count = traj.shape[2]
    quarter = lon_count // NBLK
    norm_scale = 1.0 / math.sqrt(degrees)
    step, _ = slot_step(slots)
    bands = heights // pairs
    groups = lax.axis_size("lev")

    first_slot = lax.axis_index("band") * slots
    waves_here = lax.dynamic_slice_in_dim(wave_of_slot, first_slot, slots)
    limit = jnp.broadcast_to((degrees - waves_here)[:, None, None], (slots, heights, LANES))
    weight = jnp.broadcast_to(lat_weight[:, None], (heights, LANES))
    half_turn = jnp.repeat(waves_here, 2).astype(jnp.float32) * (math.pi / lon_count)
    part_sign = 1.0 - 2.0 * (jnp.arange(slots * 2, dtype=jnp.int32) % 2).astype(jnp.float32)
    turn = jnp.stack([jnp.cos(half_turn), jnp.sin(half_turn) * part_sign])

    spec_block = pl.BlockSpec((levels, step, 2, degrees), lambda i: (0, i, 0, 0))
    leg_block = pl.BlockSpec((step, heights, degrees), lambda i: (i, 0, 0))
    limit_block = pl.BlockSpec((step, heights, LANES), lambda i: (i, 0, 0))
    turn_block = pl.BlockSpec((2, step * 2), lambda i: (0, i))
    fourier = spectral_call(
        synthesis_kernel,
        slots,
        (adj_spec, legendre, limit, weight, turn),
        [spec_block, leg_block, limit_block, pl.BlockSpec((heights, LANES), lambda i: (0, 0)), turn_block],
        jax.ShapeDtypeStruct((bands, 2, (levels + 1) * pairs, slots * 2), jnp.bfloat16),
        pl.BlockSpec((bands, 2, (levels + 1) * pairs, step * 2), lambda i: (0, 0, 0, i)),
        "synthesis",
    )
    here = lax.all_to_all(fourier, "band", split_axis=0, concat_axis=0)
    totals = here[:, :, levels * pairs :]
    totals = jnp.broadcast_to(totals[None], (groups,) + totals.shape)
    totals = lax.all_to_all(totals, "lev", split_axis=0, concat_axis=0).astype(jnp.float32)
    group_ids = jnp.arange(groups, dtype=jnp.int32)
    earlier = (group_ids < lax.axis_index("lev"))[:, None, None, None, None]
    above = jnp.sum(jnp.where(earlier, totals, 0.0), axis=0)
    whole = []
    for level in range(levels):
        value = here[:, :, level * pairs : (level + 1) * pairs].astype(jnp.float32)
        whole.append(value + lev_coef[level] * above)
        above = above + value
    whole = jnp.concatenate(whole, axis=2).astype(jnp.bfloat16)
    rows = levels * lat_rows
    here = whole.transpose(1, 2, 0, 3).reshape(rows, -1)

    table = trig_tables(wave_of_slot, lon_count, quarter)
    padded = table.shape[1]
    one = jnp.ones((here.shape[1],), jnp.bfloat16)
    sign_c = jnp.where(jnp.arange(here.shape[1], dtype=jnp.int32) % 2 == 0, one, -one)
    sign_m = jnp.where(jnp.repeat(wave_of_slot, 2) % 2 == 0, one, -one)
    signs = jnp.stack([one, sign_m * sign_c, sign_m, sign_c])
    mirrored = (here[None] * signs[:, None, :]).reshape(NBLK * rows, -1)
    grid = jnp.dot(mirrored, table, preferred_element_type=jnp.float32) * norm_scale
    grid = grid.reshape(NBLK, rows, padded)

    stored = traj.reshape(levels, pairs, 2, NBLK, quarter).transpose(3, 0, 2, 1, 4)
    stored = jnp.stack([stored[0], stored[1, ..., ::-1], stored[2], stored[3, ..., ::-1]])
    scale = jnp.exp2(traj_exp.astype(jnp.float32))
    scale = scale.reshape(levels, pairs, 2, NBLK).transpose(3, 0, 2, 1)[..., None]
    scaled = (stored.astype(jnp.float32) * scale).reshape(NBLK, levels, lat_rows, quarter)
    order_ids = jnp.arange(levels, dtype=jnp.int32)
    select = traj_order[0][None, :] == order_ids[:, None]
    value = sum(
        jnp.where(select[:, r][None, :, None, None], scaled[:, r : r + 1], 0.0)
        for r in range(levels)
    )
    value = value.reshape(NBLK, levels, 2, pairs, quarter).transpose(0, 2, 1, 3, 4)
    value = value.reshape(NBLK, rows, quarter)
    gain = jnp.pad(1.0 + jnp.tanh(value), ((0, 0), (0, 0), (0, padded - quarter)))
    forcing = (gain * grid).astype(jnp.bfloat16).reshape(NBLK * rows, padded)
    back = lax.dot_general(
        forcing, table, (((1,), (1,)), ((), ())), preferred_element_type=jnp.float32
    ).reshape(NBLK, 2, levels * pairs, -1)
    back = jnp.sum(back * signs.astype(jnp.float32)[:, None, None, :], axis=0) * norm_scale
    both = jnp.stack([back[0] + back[1], back[0] - back[1]])
    both = both.astype(jnp.bfloat16)
    width = slots * 2
    both = jnp.stack([both[:, :, band * width : (band + 1) * width] for band in range(bands)])
    returned = lax.all_to_all(both, "band", split_axis=0, concat_axis=0)
    return spectral_call(
        analysis_kernel,
        slots,
        (returned, legendre, limit, turn),
        [pl.BlockSpec((bands, 2, levels * pairs, step * 2), lambda i: (0, 0, 0, i)), leg_block, limit_block, turn_block],
        jax.ShapeDtypeStruct(adj_spec.shape, jnp.bfloat16),
        spec_block,
        "analysis",
    )


def solution(mesh):
    placed = (
        P("lev", "band", None, None),
        P(),
        P("band", None, None),
        P(),
        P("lev", "band", None),
        P("lev", "band", None),
        P("lev", None),
        P("lev"),
    )
    return jax.shard_map(
        body, mesh=mesh, in_specs=placed, out_specs=P("lev", "band", None, None), check_vma=False
    )
```

profile of v0, /device:TPU:0, one launch (start us, length us, event | category | flops | bytes accessed | tf_op | source)
XLA Modules:
  0.0 74.9 jit_solution(8231561663578233624)
XLA Ops:
  0.0 0.8 %dynamic-slice_subtract_fusion = s32[320]{0:T(512)S(1)} fusion(s32[1280]{0:T(1024)} %param.9, s32[]{:T(128)S(6)} %select_n.139), kind=kLoop, calls=%fused_computation.100 | loop fusion | flops 320 | bytes 2564 | tf_op jit(solution)/shard_map/sub | solution.py:175
  0.8 0.8 %fusion.43 = (f32[320]{0:T(512)S(1)}, f32[320]{0:T(512)S(1)}) fusion(s32[1280]{0:T(1024)} %param.9, s32[]{:T(128)S(6)} %select_n.139), kind=kLoop, calls=%fused_computation.99 | loop fusion | flops 640 | bytes 3844 | tf_op jit(solution)/shard_map/cos | solution.py:179
  2.1 0.4 broadcast_in_dim.177.limit_ref
  2.6 8.5 %synthesis.1 = bf16[4,2,10,640]{3,2,1,0:T(8,128)(2,1)S(1)} custom-call(bf16[4,320,2,1280]{3,2,1,0:T(2,128)(2,1)} %x_ref.1, bf16[320,8,1280]{2,1,0:T(8,128)(2,1)} %leg_ref.3, s32[320,8,128]{2,1,0:T(8,128)S(1)} %broadcast_in_dim.177.limit_ref, f32[8,128]{1,0:T(8,128)S(1)} %broadcast_in_dim.178.weight_ref, f32[2,640]{1,0:T(2,128)S(1)} %pad_maximum_fusion.3.turn_ref), custom_call_target="tpu_custom_call" | custom-call | tf_op jit(solution)/shard_map/synthesis/pallas_call | solution.py:122
  11.1 0.7 copy.44
  11.8 5.2 %all-to-all-start = ((bf16[4,2,10,640]{3,1,2,0:T(2,128)(2,1)}), bf16[4,2,10,640]{3,1,2,0:T(2,128)(2,1)S(1)}, u32[]{:S(2)}, u32[]{:S(2)}) async-start(bf16[4,2,10,640]{3,1,2,0:T(2,128)(2,1)} %copy.44), calls=%async_computation | async-start | bytes 204800 | tf_op jit(solution)/shard_map/all_to_all | solution.py:194
  17.3 0.3 convert_element_type.122
  17.9 0.4 reshape.556
  18.4 0.7 fusion.49
  19.4 1.0 %reverse = bf16[1,4,2,2,1408]{4,1,3,2,0:T(4,128)(2,1)S(1)} reverse(bf16[1,4,2,2,1408]{4,1,3,2,0:T(4,128)(2,1)S(1)} %bitcast.59), dimensions={4} | reverse | bytes 90112
  20.6 1.0 %reverse.1 = bf16[1,4,2,2,1408]{4,1,3,2,0:T(4,128)(2,1)S(1)} reverse(bf16[1,4,2,2,1408]{4,1,3,2,0:T(4,128)(2,1)S(1)} %bitcast.57), dimensions={4} | reverse | bytes 90112
  22.0 1.0 %slice_reduce_fusion.3 = (f32[4,4,1284]{2,1,0:T(4,128)S(1)}, f32[4,4,1284]{2,1,0:T(4,128)S(1)}, f32[4,4,1284]{2,1,0:T(4,128)S(1)}, f32[4,4,1284]{2,1,0:T(4,128)S(1)}) fusion(f32[4,4,4,1284]{3,1,2,0:T(4,128)S(1)} %convert_multiply_fusion), kind=kLoop, calls=%fused_computation.44 | loop fusion | bytes 657408 | tf_op jit(solution)/shard_map/slice | solution.py:228
  25.6 2.4 %subtract_multiply_fusion.1 = (f32[2560,128]{0,1:T(8,128)S(1)}, f32[2560,128]{0,1:T(8,128)S(1)}) fusion(f32[128]{0:T(128)S(1)} %add_convert_fusion.1, f32[2560]{0:T(1024)S(1)} %convert_element_type.122), kind=kLoop, calls=%fused_computation.23 | loop fusion | flops 17694720 | bytes 2632192 | tf_op jit(solution)/shard_map/mul | solution.py:140
  28.0 0.4 subtract_multiply_fusion.3
  28.3 5.0 %subtract_convert_fusion = bf16[2560,11,128]{0,2,1:T(8,128)(2,1)} fusion(f32[2560,128]{0,1:T(8,128)S(1)} %get-tuple-element.35, f32[2560,11]{0,1:T(8,128)S(1)} %get-tuple-element.33, f32[2560,128]{0,1:T(8,128)S(1)} %get-tuple-element.34, f32[2560,11]{0,1:T(8,128)S(1)} %get-tuple-element.32), kind=kLoop, calls=%fused_computation | loop fusion | flops 14417920 | bytes 10055680 | tf_op jit(solution)/shard_map/convert_element_type | solution.py:158
  33.7 0.8 %broadcast_in_dim.182 = bf16[8,4,2,2,640]{4,3,2,1,0:T(2,128)(2,1)} broadcast(bf16[4,2,2,640]{3,2,1,0:T(2,128)(2,1)S(1)} %copy.46), dimensions={1,2,3,4} | broadcast | bytes 184320 | tf_op jit(solution)/shard_map/broadcast_in_dim | solution.py:196
  34.4 4.9 %all-to-all-start.1 = ((bf16[8,4,2,2,640]{4,3,2,1,0:T(2,128)(2,1)}), bf16[8,4,2,2,640]{4,3,2,1,0:T(2,128)(2,1)S(1)}, u32[]{:S(2)}, u32[]{:S(2)}) async-start(bf16[8,4,2,2,640]{4,3,2,1,0:T(2,128)(2,1)} %broadcast_in_dim.182), calls=%async_computation.1 | async-start | bytes 327680 | tf_op jit(solution)/shard_map/all_to_all | solution.py:197
  39.4 7.1 %all-to-all-done.1 = bf16[8,4,2,2,640]{4,3,2,1,0:T(2,128)(2,1)S(1)} async-done(((bf16[8,4,2,2,640]{4,3,2,1,0:T(2,128)(2,1)}), bf16[8,4,2,2,640]{4,3,2,1,0:T(2,128)(2,1)S(1)}, u32[]{:S(2)}, u32[]{:S(2)}) %all-to-all-start.1) | async-done | bytes 163872 | tf_op jit(solution)/shard_map/all_to_all | solution.py:197
  46.5 0.3 select_reduce_fusion
  46.8 2.5 %fusion.21 = (bf16[4,2,2,640]{3,0,2,1:T(4,128)(2,1)S(1)}, bf16[4,2,2,640]{3,0,2,1:T(4,128)(2,1)S(1)}, bf16[4,2,2,640]{3,0,2,1:T(4,128)(2,1)S(1)}, bf16[4,2,2,640]{3,0,2,1:T(4,128)(2,1)S(1)}) fusion(f32[]{:T(128)} %bitcast.15, bf16[4,2,2,640]{3,1,2,0:T(2,128)(2,1)S(1)} %get-tuple-element.22, bf16[4,2,2,640]{3,1,2,0:T(2,128)(2,1)S(1)} %get-tuple-element.23, ...), kind=kLoop, calls=%fused_computation.60 | loop fusion | flops 194560 | bytes 204816 | tf_op jit(solution)/shard_map/convert.4
  49.4 5.5 %convolution_multiply_fusion.1 = f32[64,1408]{1,0:T(8,128)S(1)} fusion(bf16[64,2560]{1,0:T(8,128)(2,1)S(1)} %bitcast.53, bf16[2560,1408]{0,1:T(8,128)(2,1)} %bitcast.50), kind=kOutput, calls=%fused_computation.5 | convolution fusion | flops 461463552 | bytes 7897088 | tf_op jit(solution)/shard_map/dot_general | solution.py:217
  54.9 1.3 %fusion.16 = f32[2,8,2560]{2,1,0:T(8,128)S(1)} fusion(bf16[2560,1408,1,1]{0,1,3,2:T(8,128)(2,1)S(1)} %bitcast.51, f32[4,2560]{1,0:T(4,128)S(1)} %get-tuple-element.9, f32[4,16,1408]{2,1,0:T(8,128)S(1)} %bitcast.52, f32[4,16,1284]{2,1,0:T(8,128)S(1)} %tanh_add_fusion), kind=kOutput, calls=%fused_computation.24 | convolution fusion | flops 461840384 | bytes 8102912 | tf_op jit(solution)/shard_map/dot_general | solution.py:235
  56.4 8.9 %all_to_all.15.coef_ref = bf16[4,2,8,640]{3,2,1,0:T(8,128)(2,1)S(1)} all-to-all(bf16[4,2,8,640]{3,2,1,0:T(8,128)(2,1)S(1)} %pad_maximum_fusion), channel_id=1, replica_groups=mesh['band'=4,'lev'=8] {'band'}, dimensions={0} | all-to-all | bytes 163840 | tf_op jit(solution)/shard_map/all_to_all | solution.py:243
  65.2 9.7 %analysis.1 = bf16[4,320,2,1280]{3,2,1,0:T(2,128)(2,1)} custom-call(bf16[4,2,8,640]{3,2,1,0:T(8,128)(2,1)S(1)} %all_to_all.15.coef_ref, bf16[320,8,1280]{2,1,0:T(8,128)(2,1)} %leg_ref.3, s32[320,8,128]{2,1,0:T(8,128)S(1)} %broadcast_in_dim.177.limit_ref, f32[2,640]{1,0:T(2,128)S(1)} %pad_maximum_fusion.3.turn_ref), custom_call_target="tpu_custom_call" | custom-call | tf_op jit(solution)/shard_map/analysis/pallas_call | solution.py:122
  (72 shorter events, 4.9 us)
Async XLA Ops:
  0.0 2.5 %copy-start.5 = (f32[8]{0:T(128)S(1)}, f32[8]{0:T(128)}, u32[]{:S(2)}) copy-start(f32[8]{0:T(128)} %param.11) | copy-start | bytes 100
  2.6 14.4 %copy-start.2 = (s32[1280]{0:T(1024)S(1)}, s32[1280]{0:T(1024)}, u32[]{:S(2)}) copy-start(s32[1280]{0:T(1024)} %param.9) | copy-start | bytes 15364
  11.8 21.7 %all-to-all-start = ((bf16[4,2,10,640]{3,1,2,0:T(2,128)(2,1)}), bf16[4,2,10,640]{3,1,2,0:T(2,128)(2,1)S(1)}, u32[]{:S(2)}, u32[]{:S(2)}) async-start(bf16[4,2,10,640]{3,1,2,0:T(2,128)(2,1)} %copy.44), calls=%async_computation | async-start | bytes 204800 | tf_op jit(solution)/shard_map/all_to_all | solution.py:194
  17.1 1.3 %copy-start.4 = (f32[4]{0:T(128)S(1)}, f32[4]{0:T(128)}, u32[]{:S(2)}) copy-start(f32[4]{0:T(128)} %param.15) | copy-start | bytes 52
  17.1 2.0 %copy-start.1 = (bf16[4,4,5136]{2,1,0:T(4,128)(2,1)S(1)}, bf16[4,4,5136]{2,1,0:T(4,128)(2,1)}, u32[]{:S(2)}) copy-start(bf16[4,4,5136]{2,1,0:T(4,128)(2,1)} %param.12) | copy-start | bytes 493060
  17.7 4.1 %copy-start.3 = (s32[4,4,4]{2,1,0:T(4,128)S(1)}, s32[4,4,4]{2,1,0:T(4,128)}, u32[]{:S(2)}) copy-start(s32[4,4,4]{2,1,0:T(4,128)} %param.13) | copy-start | bytes 772
  23.9 0.9 %copy-start.6 = (s32[1,4]{1,0:T(1,128)S(1)}, s32[1,4]{1,0:T(1,128)}, u32[]{:S(2)}) copy-start(s32[1,4]{1,0:T(1,128)} %param.14) | copy-start | bytes 52
  34.4 12.1 %all-to-all-start.1 = ((bf16[8,4,2,2,640]{4,3,2,1,0:T(2,128)(2,1)}), bf16[8,4,2,2,640]{4,3,2,1,0:T(2,128)(2,1)S(1)}, u32[]{:S(2)}, u32[]{:S(2)}) async-start(bf16[8,4,2,2,640]{4,3,2,1,0:T(2,128)(2,1)} %broadcast_in_dim.182), calls=%async_computation.1 | async-start | bytes 327680 | tf_op jit(solution)/shard_map/all_to_all | solution.py:197
  49.4 5.5 %copy-start = (bf16[2560,11,128]{0,2,1:T(8,128)(2,1)S(1)}, bf16[2560,11,128]{0,2,1:T(8,128)(2,1)}, u32[]{:S(2)}) copy-start(bf16[2560,11,128]{0,2,1:T(8,128)(2,1)} %subtract_convert_fusion) | copy-start | bytes 21626884
where the time goes:
time: 75.6 us; the launch traced here: 74.9 us
  Pallas kernels  18.2 us (24%)
  other arithmetic  12.9 us (17%)
  local copies, waits for them, and re-layouts  10.5 us (14%)
  starting transfers between devices  10.1 us (13%)
  blocking collectives  8.87 us (12%)
  waiting for transfers between devices  7.11 us (9%)
  matrix products  6.84 us (9%)
    pallas_call x2, Pallas kernels, spectral_call(): pl.pallas_call(functools.partial(kernel, step, sub), grid=(slots // step,...  18.2 us
    all_to_all x1, blocking collectives, body(): returned = lax.all_to_all(both, 'band', split_axis=0, concat_axis=0)  8.87 us
    all_to_all x1, waiting for transfers between devices, body(): lax.all_to_all(totals, 'lev', split_axis=0, concat_axis=0)  7.11 us
    dot_general x1, matrix products, body(): jnp.dot(mirrored, table, preferred_element_type=jnp.float32) * norm_scale  5.5 us
    all_to_all x1, starting transfers between devices, body(): here = lax.all_to_all(fourier, 'band', split_axis=0, concat_axis=0)  5.19 us
    convert_element_type x1, other arithmetic, trig_tables(): return table.astype(jnp.bfloat16).reshape(wave.shape[0], blocks * LANES)  5.03 us
    all_to_all x1, starting transfers between devices, body(): lax.all_to_all(totals, 'lev', split_axis=0, concat_axis=0)  4.88 us
    mul x2, other arithmetic, cos_turn(): return -angle * series  2.77 us
  transfers between devices with their start and end apart: 2, of which 1 were waited for; matrix products, arithmetic and copies ran while one was open for 22% of the time, Pallas kernels for 0%

commit v1 on v0

v1 whole, which is shorter than its diff:
```python
import functools
import math

import jax
import jax.numpy as jnp
from jax import lax
from jax.experimental import pallas as pl
from jax.experimental.pallas import tpu as pltpu
from jax.sharding import PartitionSpec as P

NBLK = 4
LANES = 128
MESH = pl.DeviceIdType.MESH


def slot_step(slots):
    step = 64 if slots % 64 == 0 else slots
    sub = next(width for width in (32, 16, 8, 4, 2, 1) if step % width == 0)
    return step, sub


def split_parity(leg_ref, limit_ref, first, sub):
    table = leg_ref[pl.ds(first, sub)].astype(jnp.float32)
    heights, degrees = table.shape[1], table.shape[2]
    lane = lax.broadcasted_iota(jnp.int32, table.shape, 2)
    limit = jnp.concatenate([limit_ref[pl.ds(first, sub)]] * (degrees // LANES), axis=2)
    table = jnp.where(lane < limit, table, 0.0)
    even = jnp.where(lane % 2 == 0, table, 0.0)
    odd = jnp.where(lane % 2 == 0, 0.0, table)
    rows = sub * heights
    return (
        even.reshape(rows, degrees).astype(jnp.bfloat16),
        odd.reshape(rows, degrees).astype(jnp.bfloat16),
    )


def same_slot(sub, heights, levels):
    shape = (sub, heights, levels * sub * 2)
    held = lax.broadcasted_iota(jnp.int32, shape, 0)
    lane = lax.broadcasted_iota(jnp.int32, shape, 2)
    return held == (lane % (sub * 2)) // 2


def swap_pairs(value):
    lane = lax.broadcasted_iota(jnp.int32, value.shape, 1)
    width = value.shape[1]
    return jnp.where(lane % 2 == 0, pltpu.roll(value, width - 1, 1), pltpu.roll(value, 1, 1))


def synthesis_kernel(step, sub, x_ref, leg_ref, limit_ref, weight_ref, turn_ref, coef_ref, out_ref, total_ref):
    levels, degrees = x_ref.shape[0], x_ref.shape[3]
    heights = leg_ref.shape[1]
    mask = same_slot(sub, heights, levels)
    width = sub * 2
    north, south = [], []
    for first in range(0, step, sub):
        even, odd = split_parity(leg_ref, limit_ref, first, sub)
        spec = x_ref[:, pl.ds(first, sub)].reshape(levels * width, degrees)
        sums = []
        for table in (even, odd):
            cross = lax.dot_general(
                table, spec, (((1,), (1,)), ((), ())), preferred_element_type=jnp.float32
            ).reshape(sub, heights, levels * width)
            sums.append(jnp.sum(jnp.where(mask, cross, 0.0), axis=0))
        north.append(sums[0] + sums[1])
        south.append(sums[0] - sums[1])
    weight = weight_ref[...][:, :1]
    turn = turn_ref[...]
    bands = out_ref.shape[0]
    pairs = heights // bands
    for side, parts in enumerate((north, south)):
        total = None
        for level in range(levels + 1):
            if level < levels:
                lanes = slice(level * width, (level + 1) * width)
                value = jnp.concatenate([part[:, lanes] for part in parts], axis=1) * weight
                value = value * turn[0:1] + swap_pairs(value) * turn[1:2]
                held = value if total is None else value + coef_ref[level] * total
                total = value if total is None else total + value
                first, ref = (side * levels + level) * pairs, out_ref
            else:
                held, first, ref = total, side * pairs, total_ref
            sent = held.astype(jnp.bfloat16)
            for band in range(bands):
                ref[band, first : first + pairs] = sent[band * pairs : (band + 1) * pairs]


def analysis_kernel(step, sub, coef_ref, leg_ref, limit_ref, turn_ref, out_ref):
    levels, degrees = out_ref.shape[0], out_ref.shape[3]
    heights = leg_ref.shape[1]
    mask = same_slot(sub, heights, levels)
    width = sub * 2
    turn = turn_ref[...]
    held = coef_ref[...].astype(jnp.float32)
    bands = held.shape[0]
    pairs = heights // bands
    sides = []
    for side in range(2):
        values = []
        for level in range(levels):
            first = (side * levels + level) * pairs
            value = jnp.concatenate([held[band, first : first + pairs] for band in range(bands)], axis=0)
            values.append(value * turn[0:1] - swap_pairs(value) * turn[1:2])
        sides.append(values)
    for index, first in enumerate(range(0, step, sub)):
        tables = split_parity(leg_ref, limit_ref, first, sub)
        lanes = slice(index * width, (index + 1) * width)
        total = None
        for values, table in zip(sides, tables):
            row = jnp.concatenate([value[:, lanes] for value in values], axis=1)
            spread = jnp.where(mask, row[None], 0.0).reshape(sub * heights, levels * width)
            part = lax.dot_general(
                spread.astype(jnp.bfloat16),
                table,
                (((0,), (0,)), ((), ())),
                preferred_element_type=jnp.float32,
            )
            total = part if total is None else total + part
        out_ref[:, pl.ds(first, sub)] = total.astype(jnp.bfloat16).reshape(levels, sub, 2, degrees)


def spectral_call(kernel, slots, operands, specs, out_shape, out_spec, name):
    step, sub = slot_step(slots)
    return pl.pallas_call(
        functools.partial(kernel, step, sub),
        grid=(slots // step,),
        in_specs=specs,
        out_specs=out_spec,
        out_shape=out_shape,
        name=name,
        compiler_params=pltpu.CompilerParams(vmem_limit_bytes=48 * 1024 * 1024),
    )(*operands)


def cos_turn(count, period):
    left = count - jnp.floor(count * (1.0 / period)) * period
    angle = math.pi * (0.5 - jnp.abs(left * (2.0 / period) - 1.0))
    square = angle * angle
    series = 1.0
    for order in (11, 9, 7, 5, 3):
        series = 1.0 - series * square * (1.0 / (order * (order - 1)))
    return -angle * series


def fill_table(waves_ref, table_ref, lon_count):
    period = 2 * lon_count
    rows = table_ref.shape[0]
    back = 1.5 * lon_count
    row = lax.broadcasted_iota(jnp.int32, (8, LANES), 0).astype(jnp.float32)
    part = lax.broadcasted_iota(jnp.int32, (8, LANES), 1) % 2
    shift = part.astype(jnp.float32) * (lon_count // 2)

    def column(index, carry):
        lanes = pl.ds(pl.multiple_of(index * LANES, LANES), LANES)
        wave = jnp.broadcast_to(waves_ref[0:1, lanes], (8, LANES))
        near = wave * (2.0 * row + 1.0)
        near_cos, near_sin = cos_turn(near, period), cos_turn(near + back, period)
        middle = wave * (16.0 * row)
        middle_cos, middle_sin = cos_turn(middle, period), cos_turn(middle + back, period)
        fine = []
        for j in range(8):
            c, s = middle_cos[j : j + 1], middle_sin[j : j + 1]
            fine.append((near_cos * c - near_sin * s, near_sin * c + near_cos * s))
        for group in range(-(-rows // 512)):
            far = wave * (128.0 * (row + 8.0 * group)) + shift
            far_cos, far_sin = cos_turn(far, period), cos_turn(far + back, period)
            for n in range(8):
                c, s = far_cos[n : n + 1], far_sin[n : n + 1]
                for j in range(0, 8, 2):
                    first = (group * 8 + n) * 64 + j * 8
                    if first < rows:
                        block = [fine[i][0] * c - fine[i][1] * s for i in (j, j + 1)]
                        table_ref[first : first + 16, lanes] = jnp.concatenate(block).astype(jnp.bfloat16)
        return carry

    lax.fori_loop(0, table_ref.shape[1] // LANES, column, 0)


def fill_gain(traj_ref, pick_ref, gain_ref, quarter, scale):
    levels = traj_ref.shape[0]
    lon_count = traj_ref.shape[2]
    rows, padded = gain_ref.shape[1], gain_ref.shape[2]
    stored = jnp.concatenate([traj_ref[r].astype(jnp.float32) for r in range(levels)], axis=0)
    stored = stored.astype(jnp.bfloat16)
    tiles = -(-quarter // LANES)
    turned = lax.broadcasted_iota(jnp.int32, (LANES, LANES), 0)
    turned = turned + lax.broadcasted_iota(jnp.int32, (LANES, LANES), 1) == LANES - 1
    turned = jnp.where(turned, 1.0, 0.0).astype(jnp.bfloat16)
    for block in range(NBLK):
        if block % 2 == 0:
            tile = block * quarter // LANES
            skip = block * quarter - tile * LANES
        else:
            tile = ((block + 1) * quarter - 1) // LANES - (tiles - 1)
            skip = (tile + tiles) * LANES - (block + 1) * quarter
        stop = min((tile + tiles) * LANES, lon_count)
        window = stored[:, tile * LANES : stop]
        if stop < (tile + tiles) * LANES:
            fill = jnp.zeros((rows, (tile + tiles) * LANES - stop), jnp.bfloat16)
            window = jnp.concatenate([window, fill], axis=1)
        value = jnp.dot(pick_ref[block], window, preferred_element_type=jnp.float32)
        if block % 2:
            value = value.astype(jnp.bfloat16)
            stack = [value[:, t * LANES : (t + 1) * LANES] for t in reversed(range(tiles))]
            value = jnp.dot(jnp.concatenate(stack, axis=0), turned, preferred_element_type=jnp.float32)
            value = jnp.concatenate([value[t * rows : (t + 1) * rows] for t in range(tiles)], axis=1)
        value = (1.0 + jnp.tanh(value[:, skip : skip + quarter])) * scale
        gain_ref[block] = jnp.concatenate([value, jnp.zeros((rows, padded - quarter), jnp.float32)], axis=1)


def grid_kernel(
    sizes,
    mine_ref,
    total_ref,
    waves_ref,
    traj_ref,
    pick_ref,
    coef_ref,
    out_ref,
    held_ref,
    sums_ref,
    pair_ref,
    lower_ref,
    back_ref,
    table_ref,
    gain_ref,
    mine_sem,
    held_sem,
    sums_send,
    sums_sem,
    pair_send,
    lower_sem,
    back_send,
    back_sem,
):
    levels, pairs, quarter, scale = sizes
    bands, rows, width = mine_ref.shape
    lon_count = traj_ref.shape[2]
    groups = lower_ref.shape[0]
    band, lev = lax.axis_index("band"), lax.axis_index("lev")
    group, core = lev // 2, lev % 2

    def there(ahead):
        return lax.rem(band + ahead, bands)

    barrier = pltpu.get_barrier_semaphore()
    for ahead in range(bands):
        for side in range(2):
            if ahead or side:
                pl.semaphore_signal(
                    barrier,
                    inc=1,
                    device_id={"band": there(ahead), "lev": group * 2 + (core + side) % 2},
                    device_id_type=MESH,
                )
    for ahead in range(1, groups):
        pl.semaphore_signal(
            barrier,
            inc=1,
            device_id={"band": band, "lev": lax.rem(group + ahead, groups) * 2 + core},
            device_id_type=MESH,
        )
    pl.semaphore_wait(barrier, 2 * bands - 1 + groups - 1)

    sends = []
    for ahead in range(1, bands):
        sends.append(
            pltpu.make_async_remote_copy(
                src_ref=mine_ref.at[there(ahead)],
                dst_ref=held_ref.at[band],
                send_sem=mine_sem.at[ahead],
                recv_sem=held_sem.at[band],
                device_id={"band": there(ahead), "lev": lev},
                device_id_type=MESH,
            )
        )
    for ahead in range(bands):
        for side in range(2):
            if ahead or side:
                sends.append(
                    pltpu.make_async_remote_copy(
                        src_ref=total_ref.at[there(ahead)],
                        dst_ref=sums_ref.at[core, band],
                        send_sem=sums_send.at[side, ahead],
                        recv_sem=sums_sem.at[core, band],
                        device_id={"band": there(ahead), "lev": group * 2 + (core + side) % 2},
                        device_id_type=MESH,
                    )
                )
    for copy in sends:
        copy.start()
    own = [
        pltpu.make_async_copy(mine_ref.at[band], held_ref.at[band], held_sem.at[band]),
        pltpu.make_async_copy(total_ref.at[band], sums_ref.at[core, band], sums_sem.at[core, band]),
    ]
    for copy in own:
        copy.start()

    fill_gain(traj_ref, pick_ref, gain_ref, quarter, scale)

    for source in range(bands):
        for side in range(2):
            pltpu.make_async_copy(
                total_ref.at[source], sums_ref.at[side, source], sums_sem.at[side, source]
            ).wait()
    sums = sums_ref[...].astype(jnp.float32)
    sums = [jnp.concatenate([sums[side, source] for source in range(bands)], axis=1) for side in range(2)]
    pair_ref[...] = (sums[0] + sums[1]).astype(jnp.bfloat16)
    upper = []
    for ahead in range(1, groups):
        copy = pltpu.make_async_remote_copy(
            src_ref=pair_ref,
            dst_ref=lower_ref.at[group],
            send_sem=pair_send.at[ahead],
            recv_sem=lower_sem.at[group],
            device_id={"band": band, "lev": jnp.minimum(group + ahead, groups - 1) * 2 + core},
            device_id_type=MESH,
        )
        upper.append(copy)

        @pl.when(group + ahead < groups)
        def _():
            copy.start()

    fill_table(waves_ref, table_ref, lon_count)

    wave = waves_ref[...]
    part = lax.broadcasted_iota(jnp.int32, wave.shape, 1) % 2
    sign_c = 1.0 - 2.0 * part.astype(jnp.float32)
    sign_m = 1.0 - 2.0 * (wave - 2.0 * jnp.floor(wave * 0.5))
    signs = (sign_m * sign_c, sign_m, sign_c)

    def mirrored(value):
        faces = [value.astype(jnp.float32)] + [value.astype(jnp.float32) * sign for sign in signs]
        return jnp.concatenate(faces, axis=0).astype(jnp.bfloat16)

    def on_grid(value):
        return lax.dot_general(
            mirrored(value), table_ref[...], (((1,), (1,)), ((), ())), preferred_element_type=jnp.float32
        )

    for source in range(bands):
        pltpu.make_async_copy(mine_ref.at[source], held_ref.at[source], held_sem.at[source]).wait()
    grid = on_grid(jnp.concatenate([held_ref[source] for source in range(bands)], axis=1))

    above = jnp.where(core == 1, sums[0], 0.0)
    for below in range(groups - 1):

        @pl.when(below < group)
        def _():
            pltpu.make_async_copy(pair_ref, lower_ref.at[below], lower_sem.at[below]).wait()

        @pl.when(below >= group)
        def _():
            lower_ref[below] = jnp.zeros(lower_ref.shape[1:], jnp.bfloat16)

        above = above + lower_ref[below].astype(jnp.float32)
    scaled = [
        above[side * pairs : (side + 1) * pairs] * coef_ref[level]
        for side in range(2)
        for level in range(levels)
    ]
    grid = grid + on_grid(jnp.concatenate(scaled, axis=0))

    gain = jnp.concatenate([gain_ref[block] for block in range(NBLK)], axis=0)
    forcing = (gain * grid).astype(jnp.bfloat16)
    back = jnp.dot(forcing, table_ref[...], preferred_element_type=jnp.float32)
    total = back[:rows]
    for block, sign in enumerate(signs):
        total = total + back[(block + 1) * rows : (block + 2) * rows] * sign
    total = total * scale
    half = rows // 2
    both = jnp.concatenate([total[:half] + total[half:], total[:half] - total[half:]], axis=0)
    both = both.astype(jnp.bfloat16)
    for target in range(bands):
        back_ref[target] = both[:, target * width : (target + 1) * width]
    returns = [
        pltpu.make_async_remote_copy(
            src_ref=back_ref.at[there(ahead)],
            dst_ref=out_ref.at[band],
            send_sem=back_send.at[ahead],
            recv_sem=back_sem.at[band],
            device_id={"band": there(ahead), "lev": lev},
            device_id_type=MESH,
        )
        for ahead in range(1, bands)
    ]
    for copy in returns:
        copy.start()
    pltpu.make_async_copy(back_ref.at[band], out_ref.at[band], back_sem.at[band]).start()
    for source in range(bands):
        pltpu.make_async_copy(back_ref.at[source], out_ref.at[source], back_sem.at[source]).wait()
    for copy in sends + returns:
        copy.wait_send()
    for ahead, copy in enumerate(upper, 1):

        @pl.when(group + ahead < groups)
        def _():
            copy.wait_send()


def grid_call(mine, total, waves, traj, pick, coef):
    levels, lat_rows, lon_count = traj.shape
    bands, rows, width = mine.shape
    quarter = lon_count // NBLK
    padded = -(-quarter // 16) * 16
    count = waves.shape[1]
    groups = lax.axis_size("lev") // 2
    pairs = lat_rows // 2
    scale = 1.0 / math.sqrt(count // 2)
    vmem = pl.BlockSpec(memory_space=pltpu.VMEM)
    loose = pl.BlockSpec(memory_space=pl.ANY)
    dma = pltpu.SemaphoreType.DMA
    return pl.pallas_call(
        functools.partial(grid_kernel, (levels, pairs, quarter, scale)),
        in_specs=[loose, loose, vmem, vmem, vmem, pl.BlockSpec(memory_space=pltpu.SMEM)],
        out_specs=vmem,
        out_shape=jax.ShapeDtypeStruct(mine.shape, jnp.bfloat16),
        scratch_shapes=[
            pltpu.VMEM(mine.shape, jnp.bfloat16),
            pltpu.VMEM((2,) + total.shape, jnp.bfloat16),
            pltpu.VMEM((total.shape[1], count), jnp.bfloat16),
            pltpu.VMEM((groups, total.shape[1], count), jnp.bfloat16),
            pltpu.VMEM(mine.shape, jnp.bfloat16),
            pltpu.VMEM((padded, count), jnp.bfloat16),
            pltpu.VMEM((NBLK, rows, padded), jnp.float32),
            dma((bands,)),
            dma((bands,)),
            dma((2, bands)),
            dma((2, bands)),
            dma((groups,)),
            dma((groups,)),
            dma((bands,)),
            dma((bands,)),
        ],
        name="grid",
        compiler_params=pltpu.CompilerParams(
            collective_id=0, has_side_effects=True, vmem_limit_bytes=32 * 1024 * 1024
        ),
    )(mine, total, waves, traj, pick, coef)


def body(adj_spec, wave_of_slot, legendre, lat_weight, traj, traj_exp, traj_order, lev_coef):
    levels, slots, _, degrees = adj_spec.shape
    heights = legendre.shape[1]
    lat_rows = traj.shape[1]
    pairs = lat_rows // 2
    lon_count = traj.shape[2]
    quarter = lon_count // NBLK
    step, _ = slot_step(slots)
    bands = heights // pairs

    first_slot = lax.axis_index("band") * slots
    waves_here = lax.dynamic_slice_in_dim(wave_of_slot, first_slot, slots)
    limit = jnp.broadcast_to((degrees - waves_here)[:, None, None], (slots, heights, LANES))
    weight = jnp.broadcast_to(lat_weight[:, None], (heights, LANES))
    half_turn = jnp.repeat(waves_here, 2).astype(jnp.float32) * (math.pi / lon_count)
    part_sign = 1.0 - 2.0 * (jnp.arange(slots * 2, dtype=jnp.int32) % 2).astype(jnp.float32)
    turn = jnp.stack([jnp.cos(half_turn), jnp.sin(half_turn) * part_sign])

    spec_block = pl.BlockSpec((levels, step, 2, degrees), lambda i: (0, i, 0, 0))
    leg_block = pl.BlockSpec((step, heights, degrees), lambda i: (i, 0, 0))
    limit_block = pl.BlockSpec((step, heights, LANES), lambda i: (i, 0, 0))
    turn_block = pl.BlockSpec((2, step * 2), lambda i: (0, i))
    smem = pl.BlockSpec(memory_space=pltpu.SMEM)
    coef_block = pl.BlockSpec((bands, 2 * levels * pairs, step * 2), lambda i: (0, 0, i))
    total_block = pl.BlockSpec((bands, 2 * pairs, step * 2), lambda i: (0, 0, i))
    fourier, totals = spectral_call(
        synthesis_kernel,
        slots,
        (adj_spec, legendre, limit, weight, turn, lev_coef),
        [spec_block, leg_block, limit_block, pl.BlockSpec((heights, LANES), lambda i: (0, 0)), turn_block, smem],
        (
            jax.ShapeDtypeStruct((bands, 2 * levels * pairs, slots * 2), jnp.bfloat16),
            jax.ShapeDtypeStruct((bands, 2 * pairs, slots * 2), jnp.bfloat16),
        ),
        (coef_block, total_block),
        "synthesis",
    )
    waves = jnp.repeat(wave_of_slot, 2).astype(jnp.float32)[None]
    level_ids = jnp.arange(levels, dtype=jnp.int32)
    chosen = traj_order[0][None, :] == level_ids[:, None]
    own_row = jnp.arange(2, dtype=jnp.int32)[:, None] + 2 * jnp.arange(pairs, dtype=jnp.int32)[None, :]
    same_row = own_row[:, :, None] == jnp.arange(lat_rows, dtype=jnp.int32)
    chosen = chosen[None, :, None, :, None] & same_row[:, None, :, None, :]
    scales = jnp.exp2(traj_exp.astype(jnp.float32)).transpose(2, 0, 1)
    pick = jnp.where(chosen[None], scales[:, None, None, None], 0.0).astype(jnp.bfloat16)
    pick = pick.reshape(NBLK, levels * lat_rows, levels * lat_rows)
    returned = grid_call(fourier, totals, waves, traj, pick, lev_coef)
    return spectral_call(
        analysis_kernel,
        slots,
        (returned, legendre, limit, turn),
        [coef_block, leg_block, limit_block, turn_block],
        jax.ShapeDtypeStruct(adj_spec.shape, jnp.bfloat16),
        spec_block,
        "analysis",
    )


def solution(mesh):
    placed = (
        P("lev", "band", None, None),
        P(),
        P("band", None, None),
        P(),
        P("lev", "band", None),
        P("lev", "band", None),
        P("lev", None),
        P("lev"),
    )
    return jax.shard_map(
        body, mesh=mesh, in_specs=placed, out_specs=P("lev", "band", None, None), check_vma=False
    )
```

time: 75.6 us -> 49 us (0.65)
  Pallas kernels: 18.2 us -> 41.5 us
  starting transfers between devices: 10.1 us -> 0 us
  other arithmetic: 12.9 us -> 3.84 us
  blocking collectives: 8.87 us -> 0 us
  local copies, waits for them, and re-layouts: 10.5 us -> 3.06 us
  waiting for transfers between devices: 7.11 us -> 0 us
  matrix products: 6.84 us -> 0 us
    pallas_call x0 -> x1, Pallas kernels: none -> 23.2 us  [grid_call(): pl.pallas_call(functools.partial(grid_kernel, (levels, pairs, quarter, sc...]
    all_to_all x2 -> x0, starting transfers between devices: 10.1 us -> none  [the longest x1 5.19 us: body(): here = lax.all_to_all(fourier, 'band', split_axis=0, concat_axis=0)]
    all_to_all x1 -> x0, blocking collectives: 8.87 us -> none  [body(): returned = lax.all_to_all(both, 'band', split_axis=0, concat_axis=0)]
    all_to_all x2 -> x0, waiting for transfers between devices: 7.11 us -> none  [the longest x1 7.11 us: body(): lax.all_to_all(totals, 'lev', split_axis=0, concat_axis=0)]
    dot_general x2 -> x0, matrix products: 6.84 us -> none  [the longest x1 5.5 us: body(): jnp.dot(mirrored, table, preferred_element_type=jnp.float32) * norm_scale]
    convert_element_type x6 -> x2, other arithmetic: 5.1 us -> 0.71 us  [the longest x1 0.7 us: body(): waves = jnp.repeat(wave_of_slot, 2).astype(jnp.float32)[None]]
    broadcast_in_dim x24 -> x2, local copies, waits for them, and re-layouts: 3.53 us -> 0.32 us  [the longest x1 0.22 us: body(): waves = jnp.repeat(wave_of_slot, 2).astype(jnp.float32)[None]]
    mul x6 -> x1, other arithmetic: 3.03 us -> 0.01 us  [body(): 2 * jnp.arange(pairs, dtype=jnp.int32)[None, :]]
  transfers between devices with their start and end apart: 2 -> 0, of which waited for: 1 -> 0; matrix products, arithmetic and copies ran while one was open for 22% -> 0% of each run, Pallas kernels for 0% -> 0%
where the time goes in v1:
time: 49 us; the launch traced here: 48.5 us
  Pallas kernels  41.5 us (85%)
  other arithmetic  3.84 us (8%)
  local copies, waits for them, and re-layouts  3.06 us (6%)
    pallas_call x1, Pallas kernels, grid_call(): pl.pallas_call(functools.partial(grid_kernel, (levels, pairs, quarter, sc...  23.2 us
    pallas_call x2, Pallas kernels, spectral_call(): pl.pallas_call(functools.partial(kernel, step, sub), grid=(slots // step,...  18.3 us

profile of v1, /device:TPU:0, one launch (start us, length us, event | category | flops | bytes accessed | tf_op | source)
XLA Modules:
  0.0 48.5 jit_solution(11291151085297067154)
XLA Ops:
  0.0 0.7 %iota_compare_fusion.1 = pred[4,4]{1,0:T(4,128)(4,1)S(1)} fusion(s32[4]{0:T(128)} %bitcast.5), kind=kLoop, calls=%fused_computation.10 | loop fusion | flops 16 | bytes 32 | tf_op jit(solution)/shard_map/eq | solution.py:482
  0.7 0.1 iota_compare_fusion
  0.8 0.8 %dynamic-slice_subtract_fusion = s32[320]{0:T(512)S(1)} fusion(s32[1280]{0:T(1024)} %param.9, s32[]{:T(128)S(6)} %select_n.22), kind=kLoop, calls=%fused_computation.14 | loop fusion | flops 320 | bytes 2564 | tf_op jit(solution)/shard_map/sub | solution.py:455
  1.5 0.8 %fusion.5 = (f32[320]{0:T(512)S(1)}, f32[320]{0:T(512)S(1)}) fusion(s32[1280]{0:T(1024)} %param.9, s32[]{:T(128)S(6)} %select_n.22), kind=kLoop, calls=%fused_computation.13 | loop fusion | flops 640 | bytes 3844 | tf_op jit(solution)/shard_map/cos | solution.py:459
  2.3 0.7 %broadcast_in_dim.26.weight_ref = f32[8,128]{1,0:T(8,128)S(1)} broadcast(f32[8]{0:T(128)} %param.11), dimensions={0} | broadcast | bytes 4128 | tf_op jit(solution)/shard_map/broadcast_in_dim | solution.py:456
  3.1 0.7 %multiply_exponential_fusion = bf16[4,4,4]{2,1,0:T(4,128)(2,1)S(1)} fusion(s32[4,4,4]{2,1,0:T(4,128)} %param.13), kind=kLoop, calls=%fused_computation.3 | loop fusion | flops 192 | bytes 384 | tf_op jit(solution)/shard_map/exp2 | solution.py:486
  3.8 0.1 copy.11
  3.9 0.1 broadcast_and_fusion
  4.0 0.1 and.43
  4.0 0.7 %convert_element_type.49 = f32[1280]{0:T(1024)S(1)} convert(s32[1280]{0:T(1024)} %param.9) | non-fusion elementwise | flops 1280 | bytes 10240 | tf_op jit(solution)/shard_map/convert_element_type | solution.py:480
  4.7 0.1 broadcast_in_dim.54
  4.9 0.1 cos.15
  5.0 0.1 broadcast_in_dim.55
  5.1 0.1 sin.15
  5.3 0.2 broadcast_in_dim.56
  5.5 0.4 convert_element_type.50.waves_ref
  5.9 0.4 broadcast_in_dim.25.limit_ref
  6.3 0.0 copy-start.1
  6.3 0.7 %copy-done.1 = f32[4]{0:T(128)S(1)} copy-done((f32[4]{0:T(128)S(1)}, f32[4]{0:T(128)}, u32[]{:S(2)}) %copy-start.1) | copy-done | bytes 40
  7.0 0.0 copy-start
  7.0 8.6 %synthesis.1 = (bf16[4,16,640]{2,1,0:T(8,128)(2,1)S(1)}, bf16[4,4,640]{2,1,0:T(4,128)(2,1)S(1)}) custom-call(bf16[4,320,2,1280]{3,2,1,0:T(2,128)(2,1)} %x_ref.1, bf16[320,8,1280]{2,1,0:T(8,128)(2,1)} %leg_ref.3, s32[320,8,128]{2,1,0:T(8,128)S(1)} %broadcast_in_dim.25.limit_ref, f32[8,128]{1,0:T(8,128)S(1)} %broadcast_in_dim.26.weight_ref, ...), custom_call_target="tpu_custom_call" | custom-call | tf_op jit(solution)/shard_map/synthesis/pallas_call | solution.py:124
  15.6 0.0 copy-done
  15.6 23.2 %grid.1.coef_ref = bf16[4,16,640]{2,1,0:T(8,128)(2,1)S(1)} custom-call(bf16[4,16,640]{2,1,0:T(8,128)(2,1)S(1)} %get-tuple-element.7.mine_ref, bf16[4,4,640]{2,1,0:T(4,128)(2,1)S(1)} %get-tuple-element.8.total_ref, f32[1,2560]{1,0:T(1,128)S(1)} %convert_element_type.50.waves_ref, bf16[4,4,5136]{2,1,0:T(4,128)(2,1)S(1)} %copy-done, ...), custom_call_target="tpu_custom_call" | custom-call | tf_op jit(solution)/shard_map/grid/pallas_call | solution.py:414
  38.8 9.7 %analysis.1 = bf16[4,320,2,1280]{3,2,1,0:T(2,128)(2,1)} custom-call(bf16[4,16,640]{2,1,0:T(8,128)(2,1)S(1)} %grid.1.coef_ref, bf16[320,8,1280]{2,1,0:T(8,128)(2,1)} %leg_ref.3, s32[320,8,128]{2,1,0:T(8,128)S(1)} %broadcast_in_dim.25.limit_ref, f32[2,640]{1,0:T(2,128)S(1)} %pad_maximum_fusion.turn_ref), custom_call_target="tpu_custom_call" | custom-call | tf_op jit(solution)/shard_map/analysis/pallas_call | solution.py:124
  (5 shorter events, 0.0 us)
Async XLA Ops:
  6.3 0.7 %copy-start.1 = (f32[4]{0:T(128)S(1)}, f32[4]{0:T(128)}, u32[]{:S(2)}) copy-start(f32[4]{0:T(128)} %coef_ref.3) | copy-start | bytes 52
  7.0 8.6 %copy-start = (bf16[4,4,5136]{2,1,0:T(4,128)(2,1)S(1)}, bf16[4,4,5136]{2,1,0:T(4,128)(2,1)}, u32[]{:S(2)}) copy-start(bf16[4,4,5136]{2,1,0:T(4,128)(2,1)} %traj_ref.1) | copy-start | bytes 493060

commit v2 on v1

v2 whole, which is shorter than its diff:
```python
import functools
import math

import jax
import jax.numpy as jnp
from jax import lax
from jax.experimental import pallas as pl
from jax.experimental.pallas import tpu as pltpu
from jax.sharding import PartitionSpec as P

NBLK = 4
LANES = 128
MESH = pl.DeviceIdType.MESH
MIB = 1024 * 1024
TO_LANES = (((1,), (1,)), ((), ()))
VMEM = pl.BlockSpec(memory_space=pltpu.VMEM)
SMEM = pl.BlockSpec(memory_space=pltpu.SMEM)
LOOSE = pl.BlockSpec(memory_space=pl.ANY)


def in_hbm(value):
    return pltpu.with_memory_space_constraint(value, pltpu.HBM)


def slot_step(slots, heights):
    step = 64 if slots % 64 == 0 else slots
    sub = max(1, 256 // (2 * heights))
    while step % sub:
        sub -= 1
    return step, sub


def iota(shape, dim):
    return lax.broadcasted_iota(jnp.int32, shape, dim)


def swap_pairs(value):
    lane = iota(value.shape, 1)
    width = value.shape[1]
    return jnp.where(lane % 2 == 0, pltpu.roll(value, width - 1, 1), pltpu.roll(value, 1, 1))


def cos_turn(count, period):
    left = count - jnp.floor(count * (1.0 / period)) * period
    angle = math.pi * (0.5 - jnp.abs(left * (2.0 / period) - 1.0))
    square = angle * angle
    series = 1.0
    for order in (11, 9, 7, 5, 3):
        series = 1.0 - series * square * (1.0 / (order * (order - 1)))
    return -angle * series


def own_group(levels, sub, heights):
    shape = (levels * sub * 2, 2 * sub * heights)
    row, lane = iota(shape, 0), iota(shape, 1)
    return (row % (sub * 2)) // 2 == (lane % (sub * heights)) // heights


def chunk_lanes(index, step, slots):
    if step == slots:
        return slice(None)
    return pl.ds(pl.multiple_of(index * (step * 2), step * 2), step * 2)


def half_turn(waves_ref, first, step, lon_count):
    shape = (8, step * 2)
    slot = iota(shape, 1) // 2
    parts = []
    for begin in range(0, step, 8):
        wave = jnp.zeros(shape, jnp.int32)
        for s in range(begin, min(begin + 8, step)):
            wave = jnp.where(slot == s, waves_ref[first + s], wave)
        parts.append(wave)
    wave = sum(parts).astype(jnp.float32)[:1]
    sign = 1.0 - 2.0 * (iota((1, step * 2), 1) % 2).astype(jnp.float32)
    period = 2 * lon_count
    return cos_turn(wave, period), cos_turn(wave + 1.5 * lon_count, period) * sign


def masked_table(leg, limit):
    rows, degrees = leg.shape
    lane = iota((rows, LANES), 1)
    even = (lane % 2 == 0).astype(jnp.int16) == 1
    lane = lane.astype(jnp.int16)
    zero = jnp.zeros((rows, LANES), jnp.bfloat16)
    tiles = []
    for tile in range(0, degrees, LANES):
        part = jnp.where(lane + jnp.int16(tile) < limit, leg[:, tile : tile + LANES], zero)
        tiles.append(jnp.concatenate([jnp.where(even, part, zero), jnp.where(even, zero, part)], axis=0))
    return jnp.concatenate(tiles, axis=1)


def synthesis_kernel(
    lon_count,
    x_hbm,
    leg_hbm,
    waves_hbm,
    weight_hbm,
    coef_hbm,
    out_ref,
    total_ref,
    leg_ref,
    limit_ref,
    turn_ref,
    x_ref,
    kept_ref,
    waves_ref,
    weight_ref,
    coef_ref,
    x_sem,
    leg_sem,
    small_sem,
):
    levels, slots, _, degrees = x_hbm.shape
    heights = leg_hbm.shape[1]
    step, sub = slot_step(slots, heights)
    bands = out_ref.shape[0]
    pairs = heights // bands
    chunks = slots // step
    begin = lax.axis_index("band") * slots

    def copies(index):
        part = pl.ds(index * step, step)
        return (
            pltpu.make_async_copy(x_hbm.at[:, part], x_ref.at[:, part], x_sem.at[index]),
            pltpu.make_async_copy(leg_hbm.at[part], leg_ref.at[part], leg_sem.at[index]),
        )

    small = [
        pltpu.make_async_copy(waves_hbm, waves_ref, small_sem.at[0]),
        pltpu.make_async_copy(weight_hbm, weight_ref, small_sem.at[1]),
        pltpu.make_async_copy(coef_hbm, coef_ref, small_sem.at[2]),
    ]
    for copy in small:
        copy.start()
    for index in range(chunks):
        for copy in copies(index):
            copy.start()

    keep = own_group(levels, sub, heights)
    fold = (2 * heights, 2 * sub * heights)
    side, parity = iota(fold, 0) // heights, iota(fold, 1) // (sub * heights)
    sign = jnp.where(side * parity == 1, -1.0, 1.0)
    fold = jnp.where(iota(fold, 0) % heights == iota(fold, 1) % heights, sign, 0.0).astype(jnp.bfloat16)
    for copy in small:
        copy.wait()
    row = iota((2 * heights, 1), 0) % heights
    weight = jnp.zeros((2 * heights, 1), jnp.float32)
    for h in range(heights):
        weight = jnp.where(row == h, weight_ref[h], weight)

    def prepare(index, carry):
        lanes = chunk_lanes(index, step, slots)
        turn_cos, turn_sin = half_turn(waves_ref, begin + index * step, step, lon_count)
        turn_ref[0:1, lanes] = turn_cos
        turn_ref[1:2, lanes] = turn_sin
        for first in range(0, step, sub):
            here = begin + index * step + first
            limit = [jnp.full((heights, LANES), degrees - waves_ref[here + s], jnp.int32) for s in range(sub)]
            limit_ref[(index * step + first) // sub] = jnp.concatenate(limit, axis=0).astype(jnp.int16)
        return carry

    lax.fori_loop(0, chunks, prepare, 0)

    def multiply(index):
        for number, first in enumerate(range(0, step, sub)):
            local = pl.ds(index * step + first, sub)
            table = masked_table(
                leg_ref[local].reshape(sub * heights, degrees), limit_ref[(index * step + first) // sub]
            )
            spec = x_ref[:, local].reshape(levels * sub * 2, degrees)
            cross = lax.dot_general(spec, table, TO_LANES, preferred_element_type=jnp.float32)
            kept_ref[lax.rem(index, 2), number] = jnp.where(keep, cross, 0.0).astype(jnp.bfloat16)

    def finish(index):
        lanes = chunk_lanes(index, step, slots)
        turn_cos, turn_sin = turn_ref[0:1, lanes], turn_ref[1:2, lanes]
        total = None
        for level in range(levels + 1):
            if level < levels:
                rows = slice(level * sub * 2, (level + 1) * sub * 2)
                value = kept_ref[lax.rem(index, 2), :, rows].reshape(step * 2, 2 * sub * heights)
                value = lax.dot_general(fold, value, TO_LANES, preferred_element_type=jnp.float32) * weight
                value = value * turn_cos + swap_pairs(value) * turn_sin
                held = value if total is None else value + coef_ref[level] * total
                total = value if total is None else total + value
                base, ref = level * pairs, out_ref
            else:
                held, base, ref = total, 0, total_ref
            sent = held.astype(jnp.bfloat16)
            half = ref.shape[1] // 2
            for side in range(2):
                for band in range(bands):
                    first = side * heights + band * pairs
                    start = side * half + base
                    ref[band, start : start + pairs, lanes] = sent[first : first + pairs]

    for copy in copies(0):
        copy.wait()
    multiply(0)

    def chunk(index, carry):
        for copy in copies(index):
            copy.wait()
        multiply(index)
        finish(index - 1)
        return carry

    lax.fori_loop(1, chunks, chunk, 0)
    finish(chunks - 1)


def analysis_kernel(coef_ref, leg_ref, limit_ref, turn_ref, out_hbm, out_ref, part_ref, out_sem):
    levels, slots, _, degrees = out_hbm.shape
    bands = coef_ref.shape[0]
    heights = leg_ref.shape[1]
    pairs = heights // bands
    step, sub = slot_step(slots, heights)
    chunks = slots // step
    keep = own_group(levels, sub, heights)
    tile = (2 * heights, 2 * sub * heights)
    row, lane = iota(tile, 0), iota(tile, 1)
    same = (row % heights == lane % heights) & (row // heights == lane // (sub * heights))
    tile = jnp.where(same, 1.0, 0.0).astype(jnp.bfloat16)

    def copy(index):
        part = pl.ds(index * step, step)
        return pltpu.make_async_copy(out_ref.at[:, part], out_hbm.at[:, part], out_sem.at[index])

    def prepare(index):
        lanes = chunk_lanes(index, step, slots)
        turn_cos, turn_sin = turn_ref[0:1, lanes], turn_ref[1:2, lanes]
        held = coef_ref[:, :, lanes].astype(jnp.float32)
        spread = []
        for level in range(levels):
            value = []
            for side in range(2):
                for band in range(bands):
                    first = (side * levels + level) * pairs
                    value.append(held[band, first : first + pairs])
            value = jnp.concatenate(value, axis=0)
            value = (value * turn_cos - swap_pairs(value) * turn_sin).astype(jnp.bfloat16)
            spread.append(
                lax.dot_general(value, tile, (((0,), (0,)), ((), ())), preferred_element_type=jnp.float32)
            )
        for number, first in enumerate(range(0, step, sub)):
            rows = slice(first * 2, (first + sub) * 2)
            part = jnp.concatenate([value[rows] for value in spread], axis=0)
            part_ref[lax.rem(index, 2), number] = jnp.where(keep, part, 0.0).astype(jnp.bfloat16)

    def multiply(index):
        for number, first in enumerate(range(0, step, sub)):
            local = pl.ds(index * step + first, sub)
            table = masked_table(
                leg_ref[local].reshape(sub * heights, degrees), limit_ref[(index * step + first) // sub]
            )
            total = jnp.dot(part_ref[lax.rem(index, 2), number], table, preferred_element_type=jnp.float32)
            out_ref[:, local] = total.astype(jnp.bfloat16).reshape(levels, sub, 2, degrees)

    prepare(0)

    def chunk(index, carry):
        multiply(index)
        prepare(index + 1)
        copy(index).start()
        return carry

    lax.fori_loop(0, chunks - 1, chunk, 0)
    multiply(chunks - 1)
    copy(chunks - 1).start()
    for index in range(chunks):
        copy(index).wait()


def synthesis_call(adj_spec, legendre, wave_of_slot, lat_weight, lev_coef, bands, lon_count):
    levels, slots, _, degrees = adj_spec.shape
    heights = legendre.shape[1]
    step, sub = slot_step(slots, heights)
    rows = levels * heights * 2 // bands
    chunks = slots // step
    dma = pltpu.SemaphoreType.DMA
    operands = (adj_spec, legendre, wave_of_slot, lat_weight, lev_coef)
    return pl.pallas_call(
        functools.partial(synthesis_kernel, lon_count),
        in_specs=[LOOSE] * 5,
        out_specs=(VMEM,) * 5,
        out_shape=(
            pltpu.VMEM((bands, rows, slots * 2), jnp.bfloat16),
            pltpu.VMEM((bands, rows // levels, slots * 2), jnp.bfloat16),
            pltpu.VMEM(legendre.shape, jnp.bfloat16),
            pltpu.VMEM((slots // sub, sub * heights, LANES), jnp.int16),
            pltpu.VMEM((2, slots * 2), jnp.float32),
        ),
        scratch_shapes=[
            pltpu.VMEM(adj_spec.shape, jnp.bfloat16),
            pltpu.VMEM((2, step // sub, levels * sub * 2, 2 * sub * heights), jnp.bfloat16),
            pltpu.SMEM(wave_of_slot.shape, jnp.int32),
            pltpu.SMEM(lat_weight.shape, jnp.float32),
            pltpu.SMEM(lev_coef.shape, jnp.float32),
            dma((chunks,)),
            dma((chunks,)),
            dma((3,)),
        ],
        name="synthesis",
        compiler_params=pltpu.CompilerParams(vmem_limit_bytes=24 * MIB),
    )(*[in_hbm(value) for value in operands])


def analysis_call(coef, leg, limit, turn, shape):
    levels, slots, _, degrees = shape
    heights = leg.shape[1]
    step, sub = slot_step(slots, heights)
    return pl.pallas_call(
        analysis_kernel,
        in_specs=[VMEM] * 4,
        out_specs=LOOSE,
        out_shape=pltpu.HBM(shape, jnp.bfloat16),
        scratch_shapes=[
            pltpu.VMEM(shape, jnp.bfloat16),
            pltpu.VMEM((2, step // sub, levels * sub * 2, 2 * sub * heights), jnp.bfloat16),
            pltpu.SemaphoreType.DMA((slots // step,)),
        ],
        name="analysis",
        compiler_params=pltpu.CompilerParams(vmem_limit_bytes=20 * MIB),
    )(coef, leg, limit, turn)


def fill_table(waves_ref, table_ref, lon_count):
    period = 2 * lon_count
    rows = table_ref.shape[0]
    back = 1.5 * lon_count
    row = lax.broadcasted_iota(jnp.int32, (8, LANES), 0).astype(jnp.float32)
    part = lax.broadcasted_iota(jnp.int32, (8, LANES), 1) % 2
    shift = part.astype(jnp.float32) * (lon_count // 2)

    def column(index, carry):
        lanes = pl.ds(pl.multiple_of(index * LANES, LANES), LANES)
        wave = jnp.broadcast_to(waves_ref[0:1, lanes], (8, LANES))
        near = wave * (2.0 * row + 1.0)
        near_cos, near_sin = cos_turn(near, period), cos_turn(near + back, period)
        middle = wave * (16.0 * row)
        middle_cos, middle_sin = cos_turn(middle, period), cos_turn(middle + back, period)
        fine = []
        for j in range(8):
            c, s = middle_cos[j : j + 1], middle_sin[j : j + 1]
            fine.append((near_cos * c - near_sin * s, near_sin * c + near_cos * s))
        for group in range(-(-rows // 512)):
            far = wave * (128.0 * (row + 8.0 * group)) + shift
            far_cos, far_sin = cos_turn(far, period), cos_turn(far + back, period)
            for n in range(8):
                c, s = far_cos[n : n + 1], far_sin[n : n + 1]
                for j in range(0, 8, 2):
                    first = (group * 8 + n) * 64 + j * 8
                    if first < rows:
                        block = [fine[i][0] * c - fine[i][1] * s for i in (j, j + 1)]
                        table_ref[first : first + 16, lanes] = jnp.concatenate(block).astype(jnp.bfloat16)
        return carry

    lax.fori_loop(0, table_ref.shape[1] // LANES, column, 0)


def fill_waves(order_ref, waves_ref):
    wave = order_ref[...].astype(jnp.float32).reshape(order_ref.shape[0] // LANES, LANES)
    high = jnp.floor(wave * (1.0 / 256.0))
    digits = (high.astype(jnp.bfloat16), (wave - 256.0 * high).astype(jnp.bfloat16))
    for half in range(2):
        source = iota((LANES, LANES), 1) // 2 + half * (LANES // 2)
        twice = jnp.where(iota((LANES, LANES), 0) == source, 1.0, 0.0).astype(jnp.bfloat16)
        high, low = [jnp.dot(digit, twice, preferred_element_type=jnp.float32) for digit in digits]
        value = high * 256.0 + low
        for r in range(wave.shape[0]):
            first = (2 * r + half) * LANES
            waves_ref[0:1, first : first + LANES] = value[r : r + 1]


def fill_gain(traj_ref, exp_ref, order_ref, gain_ref, scale):
    levels, lat_rows, lon_count = traj_ref.shape
    quarter = lon_count // NBLK
    half = quarter // 2
    rows = levels * lat_rows
    pairs = lat_rows // 2
    padded = gain_ref.shape[1]
    stored = jnp.concatenate([traj_ref[r].astype(jnp.float32) for r in range(levels)], axis=0)
    stored = stored.astype(jnp.bfloat16)
    turned = iota((LANES, LANES), 0) + iota((LANES, LANES), 1) == LANES - 1
    turned = jnp.where(turned, 1.0, 0.0).astype(jnp.bfloat16)
    row, column = iota((rows, rows), 0), iota((rows, rows), 1)
    held = jnp.zeros((rows, rows), jnp.int32)
    for r in range(levels):
        held = jnp.where(column // lat_rows == r, order_ref[0, r], held)
    lat = 2 * (row % pairs) + row // (levels * pairs)
    hit = (held == row // pairs % levels) & (column % lat_rows == lat)
    for block in range(NBLK):
        power = jnp.zeros((rows, rows), jnp.int32)
        for r in range(levels):
            for q in range(lat_rows):
                power = jnp.where(column == r * lat_rows + q, exp_ref[r, q, block], power)
        factor = jnp.where(power < 0, jnp.where(power == -1, 0.5, 0.25), jnp.where(power == 0, 1.0, 2.0))
        factor = jnp.where(power == 2, 4.0, factor)
        pick = jnp.where(hit, factor, 0.0).astype(jnp.bfloat16)
        for reverse in range(2):
            if reverse:
                last = (block + 1) * quarter - 1
                stop = last // LANES + 1
                skip = stop * LANES - 1 - last
                tiles = -(-(skip + half) // LANES)
                tile = stop - tiles
            else:
                tile = block * quarter // LANES
                skip = block * quarter - tile * LANES
                tiles = -(-(skip + half) // LANES)
                stop = tile + tiles
            window = stored[:, tile * LANES : min(stop * LANES, lon_count)]
            if stop * LANES > lon_count:
                fill = jnp.zeros((rows, stop * LANES - lon_count), jnp.bfloat16)
                window = jnp.concatenate([window, fill], axis=1)
            value = jnp.dot(pick, window, preferred_element_type=jnp.float32)
            if reverse:
                value = value.astype(jnp.bfloat16)
                stack = [value[:, t * LANES : (t + 1) * LANES] for t in reversed(range(tiles))]
                value = jnp.dot(jnp.concatenate(stack, axis=0), turned, preferred_element_type=jnp.float32)
                value = jnp.concatenate([value[t * rows : (t + 1) * rows] for t in range(tiles)], axis=1)
            value = (1.0 + jnp.tanh(value[:, skip : skip + half])) * scale
            face = block + (NBLK if (block + reverse) % 2 else 0)
            value = jnp.concatenate([value, jnp.zeros((rows, padded - half), jnp.float32)], axis=1)
            gain_ref[face * rows : (face + 1) * rows] = value


def grid_kernel(
    sizes,
    mine_ref,
    total_ref,
    wave_of_ref,
    traj_ref,
    exp_ref,
    order_ref,
    coef_ref,
    out_ref,
    held_ref,
    sums_ref,
    pair_ref,
    lower_ref,
    back_ref,
    waves_ref,
    table_ref,
    gain_ref,
    mine_sem,
    held_sem,
    sums_send,
    sums_sem,
    pair_send,
    lower_sem,
    back_send,
    back_sem,
):
    levels, pairs, scale = sizes
    bands, rows, width = mine_ref.shape
    lon_count = traj_ref.shape[2]
    groups = lower_ref.shape[0]
    band, lev = lax.axis_index("band"), lax.axis_index("lev")
    group, core = lev // 2, lev % 2

    def there(ahead):
        return lax.rem(band + ahead, bands)

    barrier = pltpu.get_barrier_semaphore()
    for ahead in range(bands):
        for side in range(2):
            if ahead or side:
                pl.semaphore_signal(
                    barrier,
                    inc=1,
                    device_id={"band": there(ahead), "lev": group * 2 + (core + side) % 2},
                    device_id_type=MESH,
                )
    for ahead in range(1, groups):
        pl.semaphore_signal(
            barrier,
            inc=1,
            device_id={"band": band, "lev": lax.rem(group + ahead, groups) * 2 + core},
            device_id_type=MESH,
        )
    pl.semaphore_wait(barrier, 2 * bands - 1 + groups - 1)

    sends = []
    for ahead in range(1, bands):
        sends.append(
            pltpu.make_async_remote_copy(
                src_ref=mine_ref.at[there(ahead)],
                dst_ref=held_ref.at[band],
                send_sem=mine_sem.at[ahead],
                recv_sem=held_sem.at[band],
                device_id={"band": there(ahead), "lev": lev},
                device_id_type=MESH,
            )
        )
    for ahead in range(bands):
        for side in range(2):
            if ahead or side:
                sends.append(
                    pltpu.make_async_remote_copy(
                        src_ref=total_ref.at[there(ahead)],
                        dst_ref=sums_ref.at[core, band],
                        send_sem=sums_send.at[side, ahead],
                        recv_sem=sums_sem.at[core, band],
                        device_id={"band": there(ahead), "lev": group * 2 + (core + side) % 2},
                        device_id_type=MESH,
                    )
                )
    for copy in sends:
        copy.start()
    own = [
        pltpu.make_async_copy(mine_ref.at[band], held_ref.at[band], held_sem.at[band]),
        pltpu.make_async_copy(total_ref.at[band], sums_ref.at[core, band], sums_sem.at[core, band]),
    ]
    for copy in own:
        copy.start()

    fill_gain(traj_ref, exp_ref, order_ref, gain_ref, scale)
    fill_waves(wave_of_ref, waves_ref)

    for source in range(bands):
        for side in range(2):
            pltpu.make_async_copy(
                total_ref.at[source], sums_ref.at[side, source], sums_sem.at[side, source]
            ).wait()
    sums = sums_ref[...].astype(jnp.float32)
    sums = [jnp.concatenate([sums[side, source] for source in range(bands)], axis=1) for side in range(2)]
    pair_ref[...] = (sums[0] + sums[1]).astype(jnp.bfloat16)
    upper = []
    for ahead in range(1, groups):
        copy = pltpu.make_async_remote_copy(
            src_ref=pair_ref,
            dst_ref=lower_ref.at[group],
            send_sem=pair_send.at[ahead],
            recv_sem=lower_sem.at[group],
            device_id={"band": band, "lev": jnp.minimum(group + ahead, groups - 1) * 2 + core},
            device_id_type=MESH,
        )
        upper.append(copy)

        @pl.when(group + ahead < groups)
        def _():
            copy.start()

    fill_table(waves_ref, table_ref, lon_count)

    wave = waves_ref[...]
    part = iota(wave.shape, 1) % 2
    sign_c = 1.0 - 2.0 * part.astype(jnp.float32)
    sign_m = 1.0 - 2.0 * (wave - 2.0 * jnp.floor(wave * 0.5))
    phase = wave - 4.0 * jnp.floor(wave * 0.25)
    stay = jnp.where(phase == 0.0, sign_c, jnp.where(phase == 2.0, -sign_c, 0.0))
    move = jnp.where(phase == 1.0, -1.0, jnp.where(phase == 3.0, 1.0, 0.0))
    signs = (sign_m * sign_c, sign_m, sign_c)

    for source in range(bands):
        pltpu.make_async_copy(mine_ref.at[source], held_ref.at[source], held_sem.at[source]).wait()
    above = jnp.where(core == 1, sums[0], 0.0)
    for below in range(groups - 1):

        @pl.when(below < group)
        def _():
            pltpu.make_async_copy(pair_ref, lower_ref.at[below], lower_sem.at[below]).wait()

        @pl.when(below >= group)
        def _():
            lower_ref[below] = jnp.zeros(lower_ref.shape[1:], jnp.bfloat16)

        above = above + lower_ref[below].astype(jnp.float32)
    scaled = [
        above[side * pairs : (side + 1) * pairs] * coef_ref[level]
        for side in range(2)
        for level in range(levels)
    ]
    value = jnp.concatenate([held_ref[source] for source in range(bands)], axis=1).astype(jnp.float32)
    value = value + jnp.concatenate(scaled, axis=0)
    same, other = value * stay, swap_pairs(value) * move
    far, near = same + other, same - other
    faces = [value] + [value * sign for sign in signs]
    faces += [far, near * signs[0], far * signs[1], near * signs[2]]
    faces = jnp.concatenate([face.astype(jnp.bfloat16) for face in faces], axis=0)
    grid = lax.dot_general(faces, table_ref[...], TO_LANES, preferred_element_type=jnp.float32)
    forcing = (gain_ref[...] * grid).astype(jnp.bfloat16)
    back = jnp.dot(forcing, table_ref[...], preferred_element_type=jnp.float32)
    back = [back[face * rows : (face + 1) * rows] for face in range(2 * NBLK)]
    total = back[0] + back[1] * signs[0] + back[2] * signs[1] + back[3] * signs[2]
    even = back[4] + back[6] * signs[1]
    odd = back[5] * signs[0] + back[7] * signs[2]
    total = total + (even + odd) * stay + swap_pairs(even - odd) * move
    total = total * scale
    half = rows // 2
    both = jnp.concatenate([total[:half] + total[half:], total[:half] - total[half:]], axis=0)
    both = both.astype(jnp.bfloat16)
    for target in range(bands):
        back_ref[target] = both[:, target * width : (target + 1) * width]
    returns = [
        pltpu.make_async_remote_copy(
            src_ref=back_ref.at[there(ahead)],
            dst_ref=out_ref.at[band],
            send_sem=back_send.at[ahead],
            recv_sem=back_sem.at[band],
            device_id={"band": there(ahead), "lev": lev},
            device_id_type=MESH,
        )
        for ahead in range(1, bands)
    ]
    for copy in returns:
        copy.start()
    pltpu.make_async_copy(back_ref.at[band], out_ref.at[band], back_sem.at[band]).start()
    for source in range(bands):
        pltpu.make_async_copy(back_ref.at[source], out_ref.at[source], back_sem.at[source]).wait()
    for copy in sends + returns:
        copy.wait_send()
    for ahead, copy in enumerate(upper, 1):

        @pl.when(group + ahead < groups)
        def _():
            copy.wait_send()


def grid_call(mine, total, waves, traj, traj_exp, traj_order, coef):
    levels, lat_rows, lon_count = traj.shape
    bands, rows, width = mine.shape
    half = lon_count // (2 * NBLK)
    padded = -(-half // 16) * 16
    count = bands * width
    groups = lax.axis_size("lev") // 2
    pairs = lat_rows // 2
    scale = 1.0 / math.sqrt(count // 2)
    dma = pltpu.SemaphoreType.DMA
    return pl.pallas_call(
        functools.partial(grid_kernel, (levels, pairs, scale)),
        in_specs=[LOOSE, LOOSE, VMEM, VMEM, SMEM, SMEM, SMEM],
        out_specs=VMEM,
        out_shape=pltpu.VMEM(mine.shape, jnp.bfloat16),
        scratch_shapes=[
            pltpu.VMEM(mine.shape, jnp.bfloat16),
            pltpu.VMEM((2,) + total.shape, jnp.bfloat16),
            pltpu.VMEM((total.shape[1], count), jnp.bfloat16),
            pltpu.VMEM((groups, total.shape[1], count), jnp.bfloat16),
            pltpu.VMEM(mine.shape, jnp.bfloat16),
            pltpu.VMEM((1, count), jnp.float32),
            pltpu.VMEM((padded, count), jnp.bfloat16),
            pltpu.VMEM((2 * NBLK * rows, padded), jnp.float32),
            dma((bands,)),
            dma((bands,)),
            dma((2, bands)),
            dma((2, bands)),
            dma((groups,)),
            dma((groups,)),
            dma((bands,)),
            dma((bands,)),
        ],
        name="grid",
        compiler_params=pltpu.CompilerParams(
            collective_id=0, has_side_effects=True, vmem_limit_bytes=24 * MIB
        ),
    )(mine, total, waves, traj, traj_exp, traj_order, coef)


def body(adj_spec, wave_of_slot, legendre, lat_weight, traj, traj_exp, traj_order, lev_coef):
    bands = lax.axis_size("band")
    lon_count = traj.shape[2]
    fourier, totals, leg, limit, turn = synthesis_call(
        adj_spec, legendre, wave_of_slot, lat_weight, lev_coef, bands, lon_count
    )
    coef = grid_call(fourier, totals, wave_of_slot, traj, traj_exp, traj_order, lev_coef)
    return analysis_call(coef, leg, limit, turn, adj_spec.shape)


def solution(mesh):
    placed = (
        P("lev", "band", None, None),
        P(),
        P("band", None, None),
        P(),
        P("lev", "band", None),
        P("lev", "band", None),
        P("lev", None),
        P("lev"),
    )
    return jax.shard_map(
        body, mesh=mesh, in_specs=placed, out_specs=P("lev", "band", None, None), check_vma=False
    )
```

time: 49 us -> 30.8 us (0.63)
  Pallas kernels: 41.5 us -> 30.6 us
  other arithmetic: 3.84 us -> 0 us
  local copies, waits for them, and re-layouts: 3.06 us -> 0.02 us
    pallas_call x3, Pallas kernels: 41.5 us -> 30.6 us  [the longest x1 17.6 us: grid_call(): pl.pallas_call(functools.partial(grid_kernel, (levels, pairs, scale)), in...]
    broadcast_in_dim x6 -> x0, local copies, waits for them, and re-layouts: 1.63 us -> none  [the longest x1 0.73 us: body(): weight = jnp.broadcast_to(lat_weight[:, None], (heights, LANES))]
    cos x1 -> x0, other arithmetic: 0.81 us -> none  [body(): turn = jnp.stack([jnp.cos(half_turn), jnp.sin(half_turn) * part_sign])]
    sub x1 -> x0, other arithmetic: 0.77 us -> none  [body(): degrees - waves_here]
    eq x2 -> x0, other arithmetic: 0.74 us -> none  [the longest x1 0.66 us: body(): chosen = traj_order[0][None, :] == level_ids[:, None]]
    convert_element_type x2 -> x0, other arithmetic: 0.71 us -> none  [the longest x1 0.7 us: body(): waves = jnp.repeat(wave_of_slot, 2).astype(jnp.float32)[None]]
    exp2 x1 -> x0, other arithmetic: 0.71 us -> none  [body(): scales = jnp.exp2(traj_exp.astype(jnp.float32)).transpose(2, 0, 1)]
    unnamed x4 -> x10, local copies, waits for them, and re-layouts: 0.66 us -> 0.02 us
where the time goes in v2:
time: 30.8 us; the launch traced here: 30.7 us
  Pallas kernels  30.6 us (99%)
    pallas_call x1, Pallas kernels, grid_call(): pl.pallas_call(functools.partial(grid_kernel, (levels, pairs, scale)), in...  17.6 us
    pallas_call x1, Pallas kernels, synthesis_call(): pl.pallas_call(functools.partial(synthesis_kernel, lon_count), in_specs=[...  8.24 us
    pallas_call x1, Pallas kernels, analysis_call(): pl.pallas_call(analysis_kernel, in_specs=[VMEM] * 4, out_specs=LOOSE, out...  4.76 us

profile of v2, /device:TPU:0, one launch (start us, length us, event | category | flops | bytes accessed | tf_op | source)
XLA Modules:
  0.0 30.7 jit_solution(15922703047222656121)
XLA Ops:
  0.0 0.0 copy-start.3
  0.0 0.0 copy-start.1
  0.0 0.0 copy-start.4
  0.0 0.0 copy-start.2
  0.0 0.0 copy-start
  0.0 8.2 %synthesis.1 = (bf16[4,16,640]{2,1,0:T(8,128)(2,1)S(1)}, bf16[4,4,640]{2,1,0:T(4,128)(2,1)S(1)}, bf16[320,8,1280]{2,1,0:T(8,128)(2,1)S(1)}, s16[20,128,128]{2,1,0:T(8,128)(2,1)S(1)}, f32[2,640]{1,0:T(2,128)S(1)}) custom-call(bf16[4,320,2,1280]{3,2,1,0:T(2,128)(2,1)} %x_hbm.1, bf16[320,8,1280]{2,1,0:T(8,128)(2,1)} %leg_hbm.1, s32[1280]{0:T(1024)} %wave_of_ref.1, ...), custom_call_target="tpu_custom_call" | custom-call | tf_op jit(solution)/shard_map/synthesis/pallas_call | solution.py:283
  8.3 0.0 copy-done.3
  8.3 0.0 copy-done.1
  8.3 0.0 copy-done.4
  8.3 0.0 copy-done.2
  8.3 0.0 copy-done
  8.3 17.6 %grid.1.coef_ref = bf16[4,16,640]{2,1,0:T(8,128)(2,1)S(1)} custom-call(bf16[4,16,640]{2,1,0:T(8,128)(2,1)S(1)} %get-tuple-element.10.mine_ref, bf16[4,4,640]{2,1,0:T(4,128)(2,1)S(1)} %get-tuple-element.11.total_ref, s32[1280]{0:T(1024)S(1)} %copy-done.1, bf16[4,4,5136]{2,1,0:T(4,128)(2,1)S(1)} %copy-done, s32[4,4,4]{2,1,0:T(4,128)S(1)} %copy-done.2, ...), custom_call_target="tpu_custom_call" | custom-call | tf_op jit(solution)/shard_map/grid/pallas_call | solution.py:632
  25.9 4.8 %analysis.1 = bf16[4,320,2,1280]{3,2,1,0:T(2,128)(2,1)} custom-call(bf16[4,16,640]{2,1,0:T(8,128)(2,1)S(1)} %grid.1.coef_ref, bf16[320,8,1280]{2,1,0:T(8,128)(2,1)S(1)} %get-tuple-element.12.leg_ref, s16[20,128,128]{2,1,0:T(8,128)(2,1)S(1)} %get-tuple-element.13.limit_ref, f32[2,640]{1,0:T(2,128)S(1)} %get-tuple-element.14.turn_ref), custom_call_target="tpu_custom_call" | custom-call | tf_op jit(solution)/shard_map/analysis/pallas_call | solution.py:313
Async XLA Ops:
  0.0 8.3 %copy-start.3 = (f32[4]{0:T(128)S(1)}, f32[4]{0:T(128)}, u32[]{:S(2)}) copy-start(f32[4]{0:T(128)} %coef_ref.1) | copy-start | bytes 52
  0.0 8.3 %copy-start.1 = (s32[1280]{0:T(1024)S(1)}, s32[1280]{0:T(1024)}, u32[]{:S(2)}) copy-start(s32[1280]{0:T(1024)} %wave_of_ref.1) | copy-start | bytes 15364
  0.0 8.3 %copy-start.4 = (s32[1,4]{1,0:T(1,128)S(1)}, s32[1,4]{1,0:T(1,128)}, u32[]{:S(2)}) copy-start(s32[1,4]{1,0:T(1,128)} %order_ref.1) | copy-start | bytes 52
  0.0 8.3 %copy-start.2 = (s32[4,4,4]{2,1,0:T(4,128)S(1)}, s32[4,4,4]{2,1,0:T(4,128)}, u32[]{:S(2)}) copy-start(s32[4,4,4]{2,1,0:T(4,128)} %exp_ref.1) | copy-start | bytes 772
  0.0 8.3 %copy-start = (bf16[4,4,5136]{2,1,0:T(4,128)(2,1)S(1)}, bf16[4,4,5136]{2,1,0:T(4,128)(2,1)}, u32[]{:S(2)}) copy-start(bf16[4,4,5136]{2,1,0:T(4,128)(2,1)} %traj_ref.1) | copy-start | bytes 493060

commit v3 on v2

--- a/solution.py
+++ b/solution.py
@@ -90,60 +90,26 @@
     return jnp.concatenate(tiles, axis=1)
 
 
-def synthesis_kernel(
-    lon_count,
-    x_hbm,
-    leg_hbm,
-    waves_hbm,
-    weight_hbm,
-    coef_hbm,
-    out_ref,
-    total_ref,
-    leg_ref,
-    limit_ref,
-    turn_ref,
-    x_ref,
-    kept_ref,
-    waves_ref,
-    weight_ref,
-    coef_ref,
-    x_sem,
-    leg_sem,
-    small_sem,
+def synthesize(
+    lon_count, out_ref, total_ref, leg_ref, limit_ref, turn_ref, x_ref, kept_ref, waves_ref, weight_ref, coef_ref, start, arrive, first, shadow
 ):
-    levels, slots, _, degrees = x_hbm.shape
-    heights = leg_hbm.shape[1]
+    levels, slots, _, degrees = x_ref.shape
+    heights = leg_ref.shape[1]
     step, sub = slot_step(slots, heights)
     bands = out_ref.shape[0]
     pairs = heights // bands
     chunks = slots // step
     begin = lax.axis_index("band") * slots
-
-    def copies(index):
-        part = pl.ds(index * step, step)
-        return (
-            pltpu.make_async_copy(x_hbm.at[:, part], x_ref.at[:, part], x_sem.at[index]),
-            pltpu.make_async_copy(leg_hbm.at[part], leg_ref.at[part], leg_sem.at[index]),
-        )
-
-    small = [
-        pltpu.make_async_copy(waves_hbm, waves_ref, small_sem.at[0]),
-        pltpu.make_async_copy(weight_hbm, weight_ref, small_sem.at[1]),
-        pltpu.make_async_copy(coef_hbm, coef_ref, small_sem.at[2]),
-    ]
-    for copy in small:
-        copy.start()
-    for index in range(chunks):
-        for copy in copies(index):
-            copy.start()
+    depth = min(2, chunks)
+    for index in range(depth):
+        start(index)
+    first()
 
     keep = own_group(levels, sub, heights)
     fold = (2 * heights, 2 * sub * heights)
     side, parity = iota(fold, 0) // heights, iota(fold, 1) // (sub * heights)
     sign = jnp.where(side * parity == 1, -1.0, 1.0)
     fold = jnp.where(iota(fold, 0) % heights == iota(fold, 1) % heights, sign, 0.0).astype(jnp.bfloat16)
-    for copy in small:
-        copy.wait()
     row = iota((2 * heights, 1), 0) % heights
     weight = jnp.zeros((2 * heights, 1), jnp.float32)
     for h in range(heights):
@@ -161,6 +127,7 @@
         return carry
 
     lax.fori_loop(0, chunks, prepare, 0)
+    shadow()
 
     def multiply(index):
         for number, first in enumerate(range(0, step, sub)):
@@ -195,14 +162,19 @@
                     start = side * half + base
                     ref[band, start : start + pairs, lanes] = sent[first : first + pairs]
 
-    for copy in copies(0):
-        copy.wait()
-    multiply(0)
+    def take(index):
+        arrive(index)
+
+        @pl.when(index + depth < chunks)
+        def _():
+            start(index + depth)
+
+        multiply(index)
+
+    take(0)
 
     def chunk(index, carry):
-        for copy in copies(index):
-            copy.wait()
-        multiply(index)
+        take(index)
         finish(index - 1)
         return carry
 
@@ -270,40 +242,6 @@
     copy(chunks - 1).start()
     for index in range(chunks):
         copy(index).wait()
-
-
-def synthesis_call(adj_spec, legendre, wave_of_slot, lat_weight, lev_coef, bands, lon_count):
-    levels, slots, _, degrees = adj_spec.shape
-    heights = legendre.shape[1]
-    step, sub = slot_step(slots, heights)
-    rows = levels * heights * 2 // bands
-    chunks = slots // step
-    dma = pltpu.SemaphoreType.DMA
-    operands = (adj_spec, legendre, wave_of_slot, lat_weight, lev_coef)
-    return pl.pallas_call(
-        functools.partial(synthesis_kernel, lon_count),
-        in_specs=[LOOSE] * 5,
-        out_specs=(VMEM,) * 5,
-        out_shape=(
-            pltpu.VMEM((bands, rows, slots * 2), jnp.bfloat16),
-            pltpu.VMEM((bands, rows // levels, slots * 2), jnp.bfloat16),
-            pltpu.VMEM(legendre.shape, jnp.bfloat16),
-            pltpu.VMEM((slots // sub, sub * heights, LANES), jnp.int16),
-            pltpu.VMEM((2, slots * 2), jnp.float32),
-        ),
-        scratch_shapes=[
-            pltpu.VMEM(adj_spec.shape, jnp.bfloat16),
-            pltpu.VMEM((2, step // sub, levels * sub * 2, 2 * sub * heights), jnp.bfloat16),
-            pltpu.SMEM(wave_of_slot.shape, jnp.int32),
-            pltpu.SMEM(lat_weight.shape, jnp.float32),
-            pltpu.SMEM(lev_coef.shape, jnp.float32),
-            dma((chunks,)),
-            dma((chunks,)),
-            dma((3,)),
-        ],
-        name="synthesis",
-        compiler_params=pltpu.CompilerParams(vmem_limit_bytes=24 * MIB),
-    )(*[in_hbm(value) for value in operands])
 
 
 def analysis_call(coef, leg, limit, turn, shape):
@@ -428,14 +366,29 @@
 
 def grid_kernel(
     sizes,
+    x_hbm,
+    leg_hbm,
+    wave_hbm,
+    traj_hbm,
+    weight_hbm,
+    exp_hbm,
+    order_hbm,
+    coef_hbm,
+    out_ref,
+    leg_ref,
+    limit_ref,
+    turn_ref,
+    x_ref,
+    kept_ref,
     mine_ref,
     total_ref,
     wave_of_ref,
     traj_ref,
+    slot_ref,
+    weight_ref,
     exp_ref,
     order_ref,
     coef_ref,
-    out_ref,
     held_ref,
     sums_ref,
     pair_ref,
@@ -444,6 +397,9 @@
     waves_ref,
     table_ref,
     gain_ref,
+    x_sem,
+    leg_sem,
+    small_sem,
     mine_sem,
     held_sem,
     sums_send,
@@ -480,6 +436,55 @@
             device_id={"band": band, "lev": lax.rem(group + ahead, groups) * 2 + core},
             device_id_type=MESH,
         )
+    small = ((wave_hbm, slot_ref), (weight_hbm, weight_ref), (coef_hbm, coef_ref), (wave_hbm, wave_of_ref))
+    small += ((traj_hbm, traj_ref), (exp_hbm, exp_ref), (order_hbm, order_ref))
+    small = [pltpu.make_async_copy(source, ref, small_sem.at[n]) for n, (source, ref) in enumerate(small)]
+    for copy in small:
+        copy.start()
+    step, _ = slot_step(x_ref.shape[1], leg_ref.shape[1])
+
+    def copies(index):
+        part = pl.ds(index * step, step)
+        return (
+            pltpu.make_async_copy(x_hbm.at[:, part], x_ref.at[:, part], x_sem.at[index]),
+            pltpu.make_async_copy(leg_hbm.at[part], leg_ref.at[part], leg_sem.at[index]),
+        )
+
+    def start(index):
+        for copy in copies(index):
+            copy.start()
+
+    def arrive(index):
+        for copy in copies(index):
+            copy.wait()
+
+    def shadow():
+        for copy in small[3:]:
+            copy.wait()
+        fill_gain(traj_ref, exp_ref, order_ref, gain_ref, scale)
+        fill_waves(wave_of_ref, waves_ref)
+
+    def first():
+        for copy in small[:3]:
+            copy.wait()
+
+    synthesize(
+        lon_count,
+        mine_ref,
+        total_ref,
+        leg_ref,
+        limit_ref,
+        turn_ref,
+        x_ref,
+        kept_ref,
+        slot_ref,
+        weight_ref,
+        coef_ref,
+        start,
+        arrive,
+        first,
+        shadow,
+    )
     pl.semaphore_wait(barrier, 2 * bands - 1 + groups - 1)
 
     sends = []
@@ -515,9 +520,6 @@
     ]
     for copy in own:
         copy.start()
-
-    fill_gain(traj_ref, exp_ref, order_ref, gain_ref, scale)
-    fill_waves(wave_of_ref, waves_ref)
 
     for source in range(bands):
         for side in range(2):
@@ -619,30 +621,58 @@
             copy.wait_send()
 
 
-def grid_call(mine, total, waves, traj, traj_exp, traj_order, coef):
-    levels, lat_rows, lon_count = traj.shape
-    bands, rows, width = mine.shape
+def grid_call(adj_spec, legendre, wave_of_slot, traj, lat_weight, traj_exp, traj_order, lev_coef):
+    levels, slots, _, degrees = adj_spec.shape
+    heights = legendre.shape[1]
+    step, sub = slot_step(slots, heights)
+    lat_rows, lon_count = traj.shape[1:]
+    bands = lax.axis_size("band")
+    groups = lax.axis_size("lev") // 2
+    pairs = lat_rows // 2
+    rows = levels * lat_rows
+    mine = (bands, rows, slots * 2)
+    total = (bands, lat_rows, slots * 2)
+    count = bands * slots * 2
     half = lon_count // (2 * NBLK)
     padded = -(-half // 16) * 16
-    count = bands * width
-    groups = lax.axis_size("lev") // 2
-    pairs = lat_rows // 2
+    chunks = slots // step
     scale = 1.0 / math.sqrt(count // 2)
     dma = pltpu.SemaphoreType.DMA
+    bf16 = jnp.bfloat16
+    operands = (adj_spec, legendre, wave_of_slot, traj, lat_weight, traj_exp, traj_order, lev_coef)
     return pl.pallas_call(
         functools.partial(grid_kernel, (levels, pairs, scale)),
-        in_specs=[LOOSE, LOOSE, VMEM, VMEM, SMEM, SMEM, SMEM],
-        out_specs=VMEM,
-        out_shape=pltpu.VMEM(mine.shape, jnp.bfloat16),
+        in_specs=[LOOSE] * 8,
+        out_specs=(VMEM,) * 4,
+        out_shape=(
+            pltpu.VMEM(mine, bf16),
+            pltpu.VMEM(legendre.shape, bf16),
+            pltpu.VMEM((slots // sub, sub * heights, LANES), jnp.int16),
+            pltpu.VMEM((2, slots * 2), jnp.float32),
+        ),
         scratch_shapes=[
-            pltpu.VMEM(mine.shape, jnp.bfloat16),
-            pltpu.VMEM((2,) + total.shape, jnp.bfloat16),
-            pltpu.VMEM((total.shape[1], count), jnp.bfloat16),
-            pltpu.VMEM((groups, total.shape[1], count), jnp.bfloat16),
-            pltpu.VMEM(mine.shape, jnp.bfloat16),
+            pltpu.VMEM(adj_spec.shape, bf16),
+            pltpu.VMEM((2, step // sub, levels * sub * 2, 2 * sub * heights), bf16),
+            pltpu.VMEM(mine, bf16),
+            pltpu.VMEM(total, bf16),
+            pltpu.VMEM(wave_of_slot.shape, jnp.int32),
+            pltpu.VMEM(traj.shape, bf16),
+            pltpu.SMEM(wave_of_slot.shape, jnp.int32),
+            pltpu.SMEM(lat_weight.shape, jnp.float32),
+            pltpu.SMEM(traj_exp.shape, jnp.int32),
+            pltpu.SMEM(traj_order.shape, jnp.int32),
+            pltpu.SMEM(lev_coef.shape, jnp.float32),
+            pltpu.VMEM(mine, bf16),
+            pltpu.VMEM((2,) + total, bf16),
+            pltpu.VMEM((lat_rows, count), bf16),
+            pltpu.VMEM((groups, lat_rows, count), bf16),
+            pltpu.VMEM(mine, bf16),
             pltpu.VMEM((1, count), jnp.float32),
-            pltpu.VMEM((padded, count), jnp.bfloat16),
+            pltpu.VMEM((padded, count), bf16),
             pltpu.VMEM((2 * NBLK * rows, padded), jnp.float32),
+            dma((chunks,)),
+            dma((chunks,)),
+            dma((7,)),
             dma((bands,)),
             dma((bands,)),
             dma((2, bands)),
@@ -653,19 +683,14 @@
             dma((bands,)),
         ],
         name="grid",
-        compiler_params=pltpu.CompilerParams(
-            collective_id=0, has_side_effects=True, vmem_limit_bytes=24 * MIB
-        ),
-    )(mine, total, waves, traj, traj_exp, traj_order, coef)
+        compiler_params=pltpu.CompilerParams(collective_id=0, has_side_effects=True, vmem_limit_bytes=24 * MIB),
+    )(*[in_hbm(value) for value in operands])
 
 
 def body(adj_spec, wave_of_slot, legendre, lat_weight, traj, traj_exp, traj_order, lev_coef):
-    bands = lax.axis_size("band")
-    lon_count = traj.shape[2]
-    fourier, totals, leg, limit, turn = synthesis_call(
-        adj_spec, legendre, wave_of_slot, lat_weight, lev_coef, bands, lon_count
+    coef, leg, limit, turn = grid_call(
+        adj_spec, legendre, wave_of_slot, traj, lat_weight, traj_exp, traj_order, lev_coef
     )
-    coef = grid_call(fourier, totals, wave_of_slot, traj, traj_exp, traj_order, lev_coef)
     return analysis_call(coef, leg, limit, turn, adj_spec.shape)
 
 

time: 30.8 us -> 26.8 us (0.87)
  Pallas kernels: 30.6 us -> 26.6 us
    pallas_call x1 -> x0, Pallas kernels: 8.24 us -> none  [synthesis_call(): pl.pallas_call(functools.partial(synthesis_kernel, lon_count), in_specs=[...]
    pallas_call x1, Pallas kernels: 17.6 us -> 21.8 us  [grid_call(): pl.pallas_call(functools.partial(grid_kernel, (levels, pairs, scale)), in...]
where the time goes in v3:
time: 26.8 us; the launch traced here: 26.7 us
  Pallas kernels  26.6 us (99%)
    pallas_call x1, Pallas kernels, grid_call(): pl.pallas_call(functools.partial(grid_kernel, (levels, pairs, scale)), in...  21.8 us
    pallas_call x1, Pallas kernels, analysis_call(): pl.pallas_call(analysis_kernel, in_specs=[VMEM] * 4, out_specs=LOOSE, out...  4.82 us

profile of v3, /device:TPU:0, one launch (start us, length us, event | category | flops | bytes accessed | tf_op | source)
XLA Modules:
  0.0 26.7 jit_solution(17097297902570631329)
XLA Ops:
  0.0 21.8 %grid.1 = (bf16[4,16,640]{2,1,0:T(8,128)(2,1)S(1)}, bf16[320,8,1280]{2,1,0:T(8,128)(2,1)S(1)}, s16[20,128,128]{2,1,0:T(8,128)(2,1)S(1)}, f32[2,640]{1,0:T(2,128)S(1)}) custom-call(bf16[4,320,2,1280]{3,2,1,0:T(2,128)(2,1)} %x_hbm.1, bf16[320,8,1280]{2,1,0:T(8,128)(2,1)} %leg_hbm.1, s32[1280]{0:T(1024)} %wave_hbm.1, bf16[4,4,5136]{2,1,0:T(4,128)(2,1)} %traj_hbm.1, ...), custom_call_target="tpu_custom_call" | custom-call | tf_op jit(solution)/shard_map/grid/pallas_call | solution.py:643
  21.8 4.8 %analysis.1 = bf16[4,320,2,1280]{3,2,1,0:T(2,128)(2,1)} custom-call(bf16[4,16,640]{2,1,0:T(8,128)(2,1)S(1)} %get-tuple-element.9.coef_ref, bf16[320,8,1280]{2,1,0:T(8,128)(2,1)S(1)} %get-tuple-element.10.leg_ref, s16[20,128,128]{2,1,0:T(8,128)(2,1)S(1)} %get-tuple-element.11.limit_ref, f32[2,640]{1,0:T(2,128)S(1)} %get-tuple-element.12.turn_ref), custom_call_target="tpu_custom_call" | custom-call | tf_op jit(solution)/shard_map/analysis/pallas_call | solution.py:251

commit v4 on v3

--- a/solution.py
+++ b/solution.py
@@ -91,7 +91,7 @@
 
 
 def synthesize(
-    lon_count, out_ref, total_ref, leg_ref, limit_ref, turn_ref, x_ref, kept_ref, waves_ref, weight_ref, coef_ref, start, arrive, first, shadow
+    lon_count, out_ref, total_ref, leg_ref, limit_ref, turn_ref, x_ref, kept_ref, waves_ref, weight_ref, coef_ref, start, arrive, first, early
 ):
     levels, slots, _, degrees = x_ref.shape
     heights = leg_ref.shape[1]
@@ -115,7 +115,7 @@
     for h in range(heights):
         weight = jnp.where(row == h, weight_ref[h], weight)
 
-    def prepare(index, carry):
+    def prepare(index):
         lanes = chunk_lanes(index, step, slots)
         turn_cos, turn_sin = half_turn(waves_ref, begin + index * step, step, lon_count)
         turn_ref[0:1, lanes] = turn_cos
@@ -124,10 +124,8 @@
             here = begin + index * step + first
             limit = [jnp.full((heights, LANES), degrees - waves_ref[here + s], jnp.int32) for s in range(sub)]
             limit_ref[(index * step + first) // sub] = jnp.concatenate(limit, axis=0).astype(jnp.int16)
-        return carry
-
-    lax.fori_loop(0, chunks, prepare, 0)
-    shadow()
+
+    prepare(0)
 
     def multiply(index):
         for number, first in enumerate(range(0, step, sub)):
@@ -172,14 +170,29 @@
         multiply(index)
 
     take(0)
+    if chunks > 1:
+        prepare(1)
 
     def chunk(index, carry):
         take(index)
+        prepare(jnp.minimum(index + 1, chunks - 1))
         finish(index - 1)
         return carry
 
-    lax.fori_loop(1, chunks, chunk, 0)
+    if chunks > 2:
+        lax.fori_loop(1, chunks - 1, chunk, 0)
+        early()
+        chunk(chunks - 1, 0)
+    else:
+        lax.fori_loop(1, chunks, chunk, 0)
     finish(chunks - 1)
+
+
+def total_parts(slots, heights):
+    step, _ = slot_step(slots, heights)
+    chunks = slots // step
+    ends = [0, (chunks - 2) * step * 2, slots * 2] if chunks > 2 else [0, slots * 2]
+    return [slice(*pair) for pair in zip(ends, ends[1:])]
 
 
 def analysis_kernel(coef_ref, leg_ref, limit_ref, turn_ref, out_hbm, out_ref, part_ref, out_sem):
@@ -391,8 +404,8 @@
     coef_ref,
     held_ref,
     sums_ref,
-    pair_ref,
-    lower_ref,
+    pair_refs,
+    lower_refs,
     back_ref,
     waves_ref,
     table_ref,
@@ -412,7 +425,8 @@
     levels, pairs, scale = sizes
     bands, rows, width = mine_ref.shape
     lon_count = traj_ref.shape[2]
-    groups = lower_ref.shape[0]
+    groups = lower_refs[0].shape[0]
+    parts = total_parts(x_ref.shape[1], leg_ref.shape[1])
     band, lev = lax.axis_index("band"), lax.axis_index("lev")
     group, core = lev // 2, lev % 2
 
@@ -468,6 +482,65 @@
         for copy in small[:3]:
             copy.wait()
 
+    def totals_out(part):
+        lanes = parts[part]
+        return [
+            pltpu.make_async_remote_copy(
+                src_ref=total_ref.at[there(ahead), :, lanes],
+                dst_ref=sums_ref.at[core, band, :, lanes],
+                send_sem=sums_send.at[part, side, ahead],
+                recv_sem=sums_sem.at[part, core, band],
+                device_id={"band": there(ahead), "lev": group * 2 + (core + side) % 2},
+                device_id_type=MESH,
+            )
+            for ahead in range(bands)
+            for side in range(2)
+            if ahead or side
+        ]
+
+    def send_totals(part):
+        lanes = parts[part]
+        for copy in totals_out(part):
+            copy.start()
+        pltpu.make_async_copy(
+            total_ref.at[band, :, lanes], sums_ref.at[core, band, :, lanes], sums_sem.at[part, core, band]
+        ).start()
+
+    def upper_out(part):
+        return [
+            pltpu.make_async_remote_copy(
+                src_ref=pair_refs[part],
+                dst_ref=lower_refs[part].at[group],
+                send_sem=pair_send.at[part, ahead],
+                recv_sem=lower_sem.at[part, group],
+                device_id={"band": band, "lev": jnp.minimum(group + ahead, groups - 1) * 2 + core},
+                device_id_type=MESH,
+            )
+            for ahead in range(1, groups)
+        ]
+
+    def pass_up(part):
+        lanes = parts[part]
+        for source in range(bands):
+            for side in range(2):
+                pltpu.make_async_copy(
+                    total_ref.at[source, :, lanes], sums_ref.at[side, source, :, lanes], sums_sem.at[part, side, source]
+                ).wait()
+        pair = []
+        for source in range(bands):
+            both = [sums_ref[side, source, :, lanes].astype(jnp.float32) for side in range(2)]
+            pair.append((both[0] + both[1]).astype(jnp.bfloat16))
+        pair_refs[part][...] = jnp.concatenate(pair, axis=1)
+        for ahead, copy in enumerate(upper_out(part), 1):
+
+            @pl.when(group + ahead < groups)
+            def _():
+                copy.start()
+
+    def early():
+        pl.semaphore_wait(barrier, 2 * bands - 1 + groups - 1)
+        send_totals(0)
+
     synthesize(
         lon_count,
         mine_ref,
@@ -483,67 +556,30 @@
         start,
         arrive,
         first,
-        shadow,
+        early,
     )
-    pl.semaphore_wait(barrier, 2 * bands - 1 + groups - 1)
-
-    sends = []
-    for ahead in range(1, bands):
-        sends.append(
-            pltpu.make_async_remote_copy(
-                src_ref=mine_ref.at[there(ahead)],
-                dst_ref=held_ref.at[band],
-                send_sem=mine_sem.at[ahead],
-                recv_sem=held_sem.at[band],
-                device_id={"band": there(ahead), "lev": lev},
-                device_id_type=MESH,
-            )
+    if len(parts) == 1:
+        early()
+    else:
+        send_totals(1)
+    sends = [
+        pltpu.make_async_remote_copy(
+            src_ref=mine_ref.at[there(ahead)],
+            dst_ref=held_ref.at[band],
+            send_sem=mine_sem.at[ahead],
+            recv_sem=held_sem.at[band],
+            device_id={"band": there(ahead), "lev": lev},
+            device_id_type=MESH,
         )
-    for ahead in range(bands):
-        for side in range(2):
-            if ahead or side:
-                sends.append(
-                    pltpu.make_async_remote_copy(
-                        src_ref=total_ref.at[there(ahead)],
-                        dst_ref=sums_ref.at[core, band],
-                        send_sem=sums_send.at[side, ahead],
-                        recv_sem=sums_sem.at[core, band],
-                        device_id={"band": there(ahead), "lev": group * 2 + (core + side) % 2},
-                        device_id_type=MESH,
-                    )
-                )
+        for ahead in range(1, bands)
+    ]
     for copy in sends:
         copy.start()
-    own = [
-        pltpu.make_async_copy(mine_ref.at[band], held_ref.at[band], held_sem.at[band]),
-        pltpu.make_async_copy(total_ref.at[band], sums_ref.at[core, band], sums_sem.at[core, band]),
-    ]
-    for copy in own:
-        copy.start()
-
-    for source in range(bands):
-        for side in range(2):
-            pltpu.make_async_copy(
-                total_ref.at[source], sums_ref.at[side, source], sums_sem.at[side, source]
-            ).wait()
-    sums = sums_ref[...].astype(jnp.float32)
-    sums = [jnp.concatenate([sums[side, source] for source in range(bands)], axis=1) for side in range(2)]
-    pair_ref[...] = (sums[0] + sums[1]).astype(jnp.bfloat16)
-    upper = []
-    for ahead in range(1, groups):
-        copy = pltpu.make_async_remote_copy(
-            src_ref=pair_ref,
-            dst_ref=lower_ref.at[group],
-            send_sem=pair_send.at[ahead],
-            recv_sem=lower_sem.at[group],
-            device_id={"band": band, "lev": jnp.minimum(group + ahead, groups - 1) * 2 + core},
-            device_id_type=MESH,
-        )
-        upper.append(copy)
-
-        @pl.when(group + ahead < groups)
-        def _():
-            copy.start()
+    pltpu.make_async_copy(mine_ref.at[band], held_ref.at[band], held_sem.at[band]).start()
+    if len(parts) > 1:
+        pass_up(0)
+    shadow()
+    pass_up(len(parts) - 1)
 
     fill_table(waves_ref, table_ref, lon_count)
 
@@ -558,18 +594,24 @@
 
     for source in range(bands):
         pltpu.make_async_copy(mine_ref.at[source], held_ref.at[source], held_sem.at[source]).wait()
-    above = jnp.where(core == 1, sums[0], 0.0)
+    above = jnp.concatenate([sums_ref[0, source] for source in range(bands)], axis=1).astype(jnp.float32)
+    above = jnp.where(core == 1, above, 0.0)
     for below in range(groups - 1):
-
-        @pl.when(below < group)
-        def _():
-            pltpu.make_async_copy(pair_ref, lower_ref.at[below], lower_sem.at[below]).wait()
-
-        @pl.when(below >= group)
-        def _():
-            lower_ref[below] = jnp.zeros(lower_ref.shape[1:], jnp.bfloat16)
-
-        above = above + lower_ref[below].astype(jnp.float32)
+        pieces = []
+        for part, (pair_ref, lower_ref) in enumerate(zip(pair_refs, lower_refs)):
+
+            @pl.when(below < group)
+            def _():
+                pltpu.make_async_copy(pair_ref, lower_ref.at[below], lower_sem.at[part, below]).wait()
+
+            @pl.when(below >= group)
+            def _():
+                lower_ref[below] = jnp.zeros(lower_ref.shape[1:], jnp.bfloat16)
+
+            piece = lower_ref[below].astype(jnp.float32)
+            size = piece.shape[1] // bands
+            pieces.append([piece[:, source * size : (source + 1) * size] for source in range(bands)])
+        above = above + jnp.concatenate([piece[source] for source in range(bands) for piece in pieces], axis=1)
     scaled = [
         above[side * pairs : (side + 1) * pairs] * coef_ref[level]
         for side in range(2)
@@ -614,11 +656,14 @@
         pltpu.make_async_copy(back_ref.at[source], out_ref.at[source], back_sem.at[source]).wait()
     for copy in sends + returns:
         copy.wait_send()
-    for ahead, copy in enumerate(upper, 1):
-
-        @pl.when(group + ahead < groups)
-        def _():
+    for part in range(len(parts)):
+        for copy in totals_out(part):
             copy.wait_send()
+        for ahead, copy in enumerate(upper_out(part), 1):
+
+            @pl.when(group + ahead < groups)
+            def _():
+                copy.wait_send()
 
 
 def grid_call(adj_spec, legendre, wave_of_slot, traj, lat_weight, traj_exp, traj_order, lev_coef):
@@ -636,6 +681,7 @@
     half = lon_count // (2 * NBLK)
     padded = -(-half // 16) * 16
     chunks = slots // step
+    sizes = [part.stop - part.start for part in total_parts(slots, heights)]
     scale = 1.0 / math.sqrt(count // 2)
     dma = pltpu.SemaphoreType.DMA
     bf16 = jnp.bfloat16
@@ -664,8 +710,8 @@
             pltpu.SMEM(lev_coef.shape, jnp.float32),
             pltpu.VMEM(mine, bf16),
             pltpu.VMEM((2,) + total, bf16),
-            pltpu.VMEM((lat_rows, count), bf16),
-            pltpu.VMEM((groups, lat_rows, count), bf16),
+            [pltpu.VMEM((lat_rows, bands * size), bf16) for size in sizes],
+            [pltpu.VMEM((groups, lat_rows, bands * size), bf16) for size in sizes],
             pltpu.VMEM(mine, bf16),
             pltpu.VMEM((1, count), jnp.float32),
             pltpu.VMEM((padded, count), bf16),
@@ -675,10 +721,10 @@
             dma((7,)),
             dma((bands,)),
             dma((bands,)),
-            dma((2, bands)),
-            dma((2, bands)),
-            dma((groups,)),
-            dma((groups,)),
+            dma((len(sizes), 2, bands)),
+            dma((len(sizes), 2, bands)),
+            dma((len(sizes), groups)),
+            dma((len(sizes), groups)),
             dma((bands,)),
             dma((bands,)),
         ],

time: 26.8 us -> 26.2 us (0.978)
  Pallas kernels: 26.6 us -> 26 us
    pallas_call x1, Pallas kernels: 21.8 us -> 21.2 us  [grid_call(): pl.pallas_call(functools.partial(grid_kernel, (levels, pairs, scale)), in...]
where the time goes in v4:
time: 26.2 us; the launch traced here: 26 us
  Pallas kernels  26 us (99%)
    pallas_call x1, Pallas kernels, grid_call(): pl.pallas_call(functools.partial(grid_kernel, (levels, pairs, scale)), in...  21.2 us
    pallas_call x1, Pallas kernels, analysis_call(): pl.pallas_call(analysis_kernel, in_specs=[VMEM] * 4, out_specs=LOOSE, out...  4.81 us

profile of v4, /device:TPU:0, one launch (start us, length us, event | category | flops | bytes accessed | tf_op | source)
XLA Modules:
  0.0 26.0 jit_solution(7797001298767570183)
XLA Ops:
  0.0 21.2 %grid.1 = (bf16[4,16,640]{2,1,0:T(8,128)(2,1)S(1)}, bf16[320,8,1280]{2,1,0:T(8,128)(2,1)S(1)}, s16[20,128,128]{2,1,0:T(8,128)(2,1)S(1)}, f32[2,640]{1,0:T(2,128)S(1)}) custom-call(bf16[4,320,2,1280]{3,2,1,0:T(2,128)(2,1)} %x_hbm.1, bf16[320,8,1280]{2,1,0:T(8,128)(2,1)} %leg_hbm.1, s32[1280]{0:T(1024)} %wave_hbm.1, bf16[4,4,5136]{2,1,0:T(4,128)(2,1)} %traj_hbm.1, ...), custom_call_target="tpu_custom_call" | custom-call | tf_op jit(solution)/shard_map/grid/pallas_call | solution.py:689
  21.2 4.8 %analysis.1 = bf16[4,320,2,1280]{3,2,1,0:T(2,128)(2,1)} custom-call(bf16[4,16,640]{2,1,0:T(8,128)(2,1)S(1)} %get-tuple-element.9.coef_ref, bf16[320,8,1280]{2,1,0:T(8,128)(2,1)S(1)} %get-tuple-element.10.leg_ref, s16[20,128,128]{2,1,0:T(8,128)(2,1)S(1)} %get-tuple-element.11.limit_ref, f32[2,640]{1,0:T(2,128)S(1)} %get-tuple-element.12.turn_ref), custom_call_target="tpu_custom_call" | custom-call | tf_op jit(solution)/shard_map/analysis/pallas_call | solution.py:264

commit v5 on v4

--- a/solution.py
+++ b/solution.py
@@ -115,7 +115,7 @@
     for h in range(heights):
         weight = jnp.where(row == h, weight_ref[h], weight)
 
-    def prepare(index):
+    def prepare(index, carry):
         lanes = chunk_lanes(index, step, slots)
         turn_cos, turn_sin = half_turn(waves_ref, begin + index * step, step, lon_count)
         turn_ref[0:1, lanes] = turn_cos
@@ -124,8 +124,9 @@
             here = begin + index * step + first
             limit = [jnp.full((heights, LANES), degrees - waves_ref[here + s], jnp.int32) for s in range(sub)]
             limit_ref[(index * step + first) // sub] = jnp.concatenate(limit, axis=0).astype(jnp.int16)
-
-    prepare(0)
+        return carry
+
+    lax.fori_loop(0, chunks, prepare, 0)
 
     def multiply(index):
         for number, first in enumerate(range(0, step, sub)):
@@ -167,16 +168,13 @@
         def _():
             start(index + depth)
 
-        multiply(index)
-
     take(0)
-    if chunks > 1:
-        prepare(1)
+    multiply(0)
 
     def chunk(index, carry):
         take(index)
-        prepare(jnp.minimum(index + 1, chunks - 1))
         finish(index - 1)
+        multiply(index)
         return carry
 
     if chunks > 2:
@@ -434,22 +432,6 @@
         return lax.rem(band + ahead, bands)
 
     barrier = pltpu.get_barrier_semaphore()
-    for ahead in range(bands):
-        for side in range(2):
-            if ahead or side:
-                pl.semaphore_signal(
-                    barrier,
-                    inc=1,
-                    device_id={"band": there(ahead), "lev": group * 2 + (core + side) % 2},
-                    device_id_type=MESH,
-                )
-    for ahead in range(1, groups):
-        pl.semaphore_signal(
-            barrier,
-            inc=1,
-            device_id={"band": band, "lev": lax.rem(group + ahead, groups) * 2 + core},
-            device_id_type=MESH,
-        )
     small = ((wave_hbm, slot_ref), (weight_hbm, weight_ref), (coef_hbm, coef_ref), (wave_hbm, wave_of_ref))
     small += ((traj_hbm, traj_ref), (exp_hbm, exp_ref), (order_hbm, order_ref))
     small = [pltpu.make_async_copy(source, ref, small_sem.at[n]) for n, (source, ref) in enumerate(small)]
@@ -479,6 +461,22 @@
         fill_waves(wave_of_ref, waves_ref)
 
     def first():
+        for ahead in range(bands):
+            for side in range(2):
+                if ahead or side:
+                    pl.semaphore_signal(
+                        barrier,
+                        inc=1,
+                        device_id={"band": there(ahead), "lev": group * 2 + (core + side) % 2},
+                        device_id_type=MESH,
+                    )
+        for ahead in range(1, groups):
+            pl.semaphore_signal(
+                barrier,
+                inc=1,
+                device_id={"band": band, "lev": lax.rem(group + ahead, groups) * 2 + core},
+                device_id_type=MESH,
+            )
         for copy in small[:3]:
             copy.wait()
 

time: 26.2 us -> 25.6 us (0.977)
  Pallas kernels: 26 us -> 25.4 us
    pallas_call x1, Pallas kernels: 21.2 us -> 20.6 us  [grid_call(): pl.pallas_call(functools.partial(grid_kernel, (levels, pairs, scale)), in...]
where the time goes in v5:
time: 25.6 us; the launch traced here: 25.4 us
  Pallas kernels  25.4 us (99%)
    pallas_call x1, Pallas kernels, grid_call(): pl.pallas_call(functools.partial(grid_kernel, (levels, pairs, scale)), in...  20.6 us
    pallas_call x1, Pallas kernels, analysis_call(): pl.pallas_call(analysis_kernel, in_specs=[VMEM] * 4, out_specs=LOOSE, out...  4.82 us

profile of v5, /device:TPU:0, one launch (start us, length us, event | category | flops | bytes accessed | tf_op | source)
XLA Modules:
  0.0 25.4 jit_solution(1424274617385075266)
XLA Ops:
  0.0 20.6 %grid.1 = (bf16[4,16,640]{2,1,0:T(8,128)(2,1)S(1)}, bf16[320,8,1280]{2,1,0:T(8,128)(2,1)S(1)}, s16[20,128,128]{2,1,0:T(8,128)(2,1)S(1)}, f32[2,640]{1,0:T(2,128)S(1)}) custom-call(bf16[4,320,2,1280]{3,2,1,0:T(2,128)(2,1)} %x_hbm.1, bf16[320,8,1280]{2,1,0:T(8,128)(2,1)} %leg_hbm.1, s32[1280]{0:T(1024)} %wave_hbm.1, bf16[4,4,5136]{2,1,0:T(4,128)(2,1)} %traj_hbm.1, ...), custom_call_target="tpu_custom_call" | custom-call | tf_op jit(solution)/shard_map/grid/pallas_call | solution.py:687
  20.6 4.8 %analysis.1 = bf16[4,320,2,1280]{3,2,1,0:T(2,128)(2,1)} custom-call(bf16[4,16,640]{2,1,0:T(8,128)(2,1)S(1)} %get-tuple-element.9.coef_ref, bf16[320,8,1280]{2,1,0:T(8,128)(2,1)S(1)} %get-tuple-element.10.leg_ref, s16[20,128,128]{2,1,0:T(8,128)(2,1)S(1)} %get-tuple-element.11.limit_ref, f32[2,640]{1,0:T(2,128)S(1)} %get-tuple-element.12.turn_ref), custom_call_target="tpu_custom_call" | custom-call | tf_op jit(solution)/shard_map/analysis/pallas_call | solution.py:262

commit v6 on v5

--- a/solution.py
+++ b/solution.py
@@ -274,7 +274,7 @@
     )(coef, leg, limit, turn)
 
 
-def fill_table(waves_ref, table_ref, lon_count):
+def fill_table(waves_ref, table_ref, lon_count, first, last):
     period = 2 * lon_count
     rows = table_ref.shape[0]
     back = 1.5 * lon_count
@@ -305,7 +305,7 @@
                         table_ref[first : first + 16, lanes] = jnp.concatenate(block).astype(jnp.bfloat16)
         return carry
 
-    lax.fori_loop(0, table_ref.shape[1] // LANES, column, 0)
+    lax.fori_loop(first, last, column, 0)
 
 
 def fill_waves(order_ref, waves_ref):
@@ -529,7 +529,7 @@
             both = [sums_ref[side, source, :, lanes].astype(jnp.float32) for side in range(2)]
             pair.append((both[0] + both[1]).astype(jnp.bfloat16))
         pair_refs[part][...] = jnp.concatenate(pair, axis=1)
-        for ahead, copy in enumerate(upper_out(part), 1):
+        for ahead, copy in reversed(list(enumerate(upper_out(part), 1))):
 
             @pl.when(group + ahead < groups)
             def _():
@@ -577,9 +577,11 @@
     if len(parts) > 1:
         pass_up(0)
     shadow()
+    columns = table_ref.shape[1] // LANES
+    ready = columns * 10 // 20
+    fill_table(waves_ref, table_ref, lon_count, 0, ready)
     pass_up(len(parts) - 1)
-
-    fill_table(waves_ref, table_ref, lon_count)
+    fill_table(waves_ref, table_ref, lon_count, ready, columns)
 
     wave = waves_ref[...]
     part = iota(wave.shape, 1) % 2

time: 25.6 us -> 24.8 us (0.969)
  Pallas kernels: 25.4 us -> 24.7 us
    pallas_call x1, Pallas kernels: 20.6 us -> 19.8 us  [grid_call(): pl.pallas_call(functools.partial(grid_kernel, (levels, pairs, scale)), in...]
where the time goes in v6:
time: 24.8 us; the launch traced here: 24.7 us
  Pallas kernels  24.7 us (100%)
    pallas_call x1, Pallas kernels, grid_call(): pl.pallas_call(functools.partial(grid_kernel, (levels, pairs, scale)), in...  19.8 us
    pallas_call x1, Pallas kernels, analysis_call(): pl.pallas_call(analysis_kernel, in_specs=[VMEM] * 4, out_specs=LOOSE, out...  4.82 us

profile of v6, /device:TPU:0, one launch (start us, length us, event | category | flops | bytes accessed | tf_op | source)
XLA Modules:
  0.0 24.7 jit_solution(3952303784388766351)
XLA Ops:
  0.0 19.8 %grid.1 = (bf16[4,16,640]{2,1,0:T(8,128)(2,1)S(1)}, bf16[320,8,1280]{2,1,0:T(8,128)(2,1)S(1)}, s16[20,128,128]{2,1,0:T(8,128)(2,1)S(1)}, f32[2,640]{1,0:T(2,128)S(1)}) custom-call(bf16[4,320,2,1280]{3,2,1,0:T(2,128)(2,1)} %x_hbm.1, bf16[320,8,1280]{2,1,0:T(8,128)(2,1)} %leg_hbm.1, s32[1280]{0:T(1024)} %wave_hbm.1, bf16[4,4,5136]{2,1,0:T(4,128)(2,1)} %traj_hbm.1, ...), custom_call_target="tpu_custom_call" | custom-call | tf_op jit(solution)/shard_map/grid/pallas_call | solution.py:689
  19.9 4.8 %analysis.1 = bf16[4,320,2,1280]{3,2,1,0:T(2,128)(2,1)} custom-call(bf16[4,16,640]{2,1,0:T(8,128)(2,1)S(1)} %get-tuple-element.9.coef_ref, bf16[320,8,1280]{2,1,0:T(8,128)(2,1)S(1)} %get-tuple-element.10.leg_ref, s16[20,128,128]{2,1,0:T(8,128)(2,1)S(1)} %get-tuple-element.11.limit_ref, f32[2,640]{1,0:T(2,128)S(1)} %get-tuple-element.12.turn_ref), custom_call_target="tpu_custom_call" | custom-call | tf_op jit(solution)/shard_map/analysis/pallas_call | solution.py:262
